TPU v7x, 1024 devices: a whole 4x4x32 slice. The times are simulated.
1024 devices in a mesh: tiles: 256 (over x, z, core), strip: 4 (over y).
Axes of the slice: x: 4, y: 4, z: 32, core: 2. Of those that a mesh axis runs over, the one named last changes fastest.
Arguments:
- fields: float32 [256, 4, 3, 3, 4, 8100], P('tiles', 'strip'), may hold values from -6 to 6
- wet_land: int32 [256, 4, 3, 8100], P('tiles', 'strip'), may hold values from 0 to 1, as said below
- links: int32 [256, 4, 3, 4, 4], P('tiles', 'strip'), may hold values from -1 to 3, as said below
- surface_diagonal: float32 [256, 4, 3, 8100], P('tiles', 'strip'), may hold values from 0.25 to 2
- spread: float32 [3, 4], replicated, may hold values from 0.02 to 0.2
- mixing: float32 [4], replicated, may hold values from 0.02 to 0.2
- thickness: float32 [4], replicated, may hold values from 0.5 to 2
Outputs:
- adjoint_fields: float32 [256, 4, 3, 3, 4, 8100], P('tiles', 'strip')
- surface_solution: float32 [256, 4, 3, 8100], P('tiles', 'strip')
- surface_residual: float32 [256, 4, 3, 8100], P('tiles', 'strip')
Inputs may be any that keep to these rules, and one draw needn't show every extreme that they name: wet_land is 1 on most cells of the first 1 to 3 slots of each device and 0 on all cells of its other slots. Offsets dt and ds are -1, 0 or 1; on the west and east sides dt is -1 and 1, on the south and north sides ds is -1 and 1; a partner slot is -1 or a slot that holds wet cells; links are mutual: side e of slot k pairs with side e XOR 1 of its partner, whose entry points back with opposite offsets and rotation code (4 - code) mod 4; an empty slot has no links; rotation codes are 0 to 3.
All inputs are finite; a program needn't handle non-finite values.
Results may differ from a plain program's by a relative error of at most 0.00027.
Values sent between devices are 32-bit elements; how exact they have to be, the bound alone decides.
A program may use at most 64 MiB of HBM per device.

v0:
```python
import jax
import jax.numpy as jnp
import numpy as np
from jax import lax
from jax.sharding import Mesh
from jax.sharding import PartitionSpec as P

TILE = 90
SLOTS = 3
ITERS = 2
TILES_STRIP = ("tiles_0", "tiles_1", "tiles_2", "strip")
TILES = ("tiles_0", "tiles_1", "tiles_2")


OPPOSITE = np.array([1, 0, 3, 2], np.int32)


def over_axes(value, axes):
    for axis in axes:
        value = lax.psum(value, axis)
    return value


def extended(value, sides, width):
    for axis, dim in sides:
        peers, length = (lax.axis_size(axis), value.shape[dim])
        up = [(i, (i + 1) % peers) for i in range(peers)]
        down = [(j, i) for i, j in up]
        last = lax.slice_in_dim(value, length - width, length, axis=dim)
        leading = lax.slice_in_dim(value, 0, width, axis=dim)
        before = lax.ppermute(last, axis, up)
        after = lax.ppermute(leading, axis, down)
        value = jnp.concatenate([before, value, after], axis=dim)
    return value


def rim_rows(values, width):
    west_rim = values[..., ::width]
    east_rim = values[..., width - 1 :: width]
    south_rim = values[..., :width]
    north_rim = values[..., -width:]
    return jnp.concatenate([west_rim, east_rim, south_rim, north_rim], axis=-1)


def beside_values(values, rims, width):
    cells_total = values.shape[-1]
    leading = values.shape[:-1]
    places = jnp.arange(cells_total, dtype=jnp.int32)
    column_index = places % width
    row_index = places // width
    west_full = jnp.broadcast_to(rims[..., 0, :, None], leading + (width, width)).reshape(
        leading + (cells_total,)
    )
    east_full = jnp.broadcast_to(rims[..., 1, :, None], leading + (width, width)).reshape(
        leading + (cells_total,)
    )
    south_full = jnp.broadcast_to(rims[..., 2, None, :], leading + (width, width)).reshape(
        leading + (cells_total,)
    )
    north_full = jnp.broadcast_to(rims[..., 3, None, :], leading + (width, width)).reshape(
        leading + (cells_total,)
    )
    zero_cell = jnp.zeros(leading + (1,), jnp.float32)
    zero_line = jnp.zeros(leading + (width,), jnp.float32)
    west_side = jnp.where(
        column_index == 0, west_full, jnp.concatenate([zero_cell, values[..., :-1]], -1)
    )
    east_side = jnp.where(
        column_index == width - 1, east_full, jnp.concatenate([values[..., 1:], zero_cell], -1)
    )
    south_side = jnp.where(
        row_index == 0, south_full, jnp.concatenate([zero_line, values[..., :-width]], -1)
    )
    north_side = jnp.where(
        row_index == width - 1, north_full, jnp.concatenate([values[..., width:], zero_line], -1)
    )
    return (west_side, east_side, south_side, north_side)


def orient(picked, links, vector):
    code = links[..., 3]
    partner = links[..., 2]
    lead = code.ndim
    extra = picked.ndim - lead
    tail_shape = code.shape + (1,) * extra
    flipped = jnp.where((code != 0).reshape(tail_shape), jnp.flip(picked, -1), picked)
    flipped = flipped * (partner >= 0).astype(jnp.float32).reshape(tail_shape)
    if vector:
        turn_shape = code.shape + (1,) * (extra - 1)
        cosine_part = ((code == 0).astype(jnp.float32) - (code == 2).astype(jnp.float32)).reshape(
            turn_shape
        )
        sine_part = ((code == 1).astype(jnp.float32) - (code == 3).astype(jnp.float32)).reshape(
            turn_shape
        )
        eastward = jnp.take(flipped, 0, axis=lead)
        northward = jnp.take(flipped, 1, axis=lead)
        scalar_part = jnp.take(flipped, 2, axis=lead)
        flipped = jnp.stack(
            [
                cosine_part * eastward + sine_part * northward,
                cosine_part * northward - sine_part * eastward,
                scalar_part,
            ],
            axis=lead,
        )
    return jnp.moveaxis(flipped, lead - 1, -2)


def slab_step(fields, wet, rims, spread, mixing, thickness, width):
    wet_cells = wet[..., None, None, :]
    masked = fields * wet_cells
    west_side, east_side, south_side, north_side = beside_values(masked, rims, width)
    flat_term = west_side + east_side + south_side + north_side - 4.0 * masked
    above = jnp.concatenate([masked[..., 1:, :], masked[..., -1:, :]], axis=-2)
    below = jnp.concatenate([masked[..., :1, :], masked[..., :-1, :]], axis=-2)
    column_term = above + below - 2.0 * masked
    updated = wet_cells * (masked + spread[:, :, None] * flat_term + mixing[:, None] * column_term)
    flux = 0.5 * (
        east_side[..., 0, :, :]
        - west_side[..., 0, :, :]
        + north_side[..., 1, :, :]
        - south_side[..., 1, :, :]
    )
    source = wet * jnp.sum(thickness[:, None] * flux, axis=-2)
    return (updated, source)


def surface_apply(values, wet, rims, diagonal, width):
    west_side, east_side, south_side, north_side = beside_values(values, rims, width)
    return wet * ((4.0 + diagonal) * values - (west_side + east_side + south_side + north_side))


def pick_local(tile_packs, flat_index):
    opposite = jnp.broadcast_to(jnp.asarray(OPPOSITE)[None, :], flat_index.shape)
    return tile_packs[flat_index, ..., opposite, :]


def paired_totals(residual, image):
    return (
        over_axes(jnp.sum(residual * residual), TILES_STRIP),
        over_axes(jnp.sum(residual * image), TILES_STRIP),
    )


def on_device(fields, wet_land, links, surface_diagonal, spread, mixing, thickness):
    local_fields = fields[0, 0]
    wet = wet_land[0, 0].astype(jnp.float32)
    local_links = links[0, 0]
    diagonal = surface_diagonal[0, 0]
    group_shift = local_links[..., 0]
    strip_shift = local_links[..., 1]
    partner = jnp.maximum(local_links[..., 2], 0)
    near_index = ((group_shift + 1) * 3 + strip_shift + 1) * SLOTS + partner
    masked = local_fields * wet[:, None, None, :]
    slab_pack = rim_rows(masked, TILE)[None, None]
    neighbours = extended(slab_pack, ((TILES, 0), ("strip", 1)), 1)
    slab_packs = neighbours.reshape((-1,) + masked.shape[1:-1] + (4, TILE))
    picked = pick_local(slab_packs, near_index)
    slab_rims = orient(picked, local_links, True)
    updated, source = slab_step(local_fields, wet, slab_rims, spread, mixing, thickness, TILE)

    def surface_image(values):
        surface_pack = rim_rows(values, TILE)[None, None]
        surface_near = extended(surface_pack, ((TILES, 0), ("strip", 1)), 1)
        surface_packs = surface_near.reshape((-1, 4, TILE))
        rims = orient(pick_local(surface_packs, near_index), local_links, False)
        return surface_apply(values, wet, rims, diagonal, TILE)

    solution = jnp.zeros_like(source)
    residual = source
    image = surface_image(residual)
    norm_now, product = paired_totals(residual, image)
    alpha = norm_now / product
    direction = residual
    conjugate = image
    for iteration in range(ITERS):
        solution = solution + alpha * direction
        residual = residual - alpha * conjugate
        if iteration + 1 < ITERS:
            image = surface_image(residual)
            norm_next, product = paired_totals(residual, image)
            ratio = norm_next / norm_now
            alpha = norm_next / (product - ratio * norm_next / alpha)
            direction = residual + ratio * direction
            conjugate = image + ratio * conjugate
            norm_now = norm_next
    return (updated[None, None], solution[None, None], residual[None, None])


def solution(mesh):
    torus = Mesh(
        mesh.devices.reshape(4, 32, 2, mesh.shape["strip"]),
        ("tiles_0", "tiles_1", "tiles_2", "strip"),
    )
    return jax.shard_map(
        on_device,
        mesh=torus,
        in_specs=(
            P(TILES, "strip", None, None, None, None),
            P(TILES, "strip", None, None),
            P(TILES, "strip", None, None, None),
            P(TILES, "strip", None, None),
            P(),
            P(),
            P(),
        ),
        out_specs=(
            P(TILES, "strip", None, None, None, None),
            P(TILES, "strip", None, None),
            P(TILES, "strip", None, None),
        ),
        check_vma=False,
    )
```

profile of v0, /device:TPU:1, one launch (start us, length us, event | category | flops | bytes accessed | tf_op | source)
XLA Modules:
  0.0 273.2 jit_solution(17591021525347701376)
XLA Ops:
  5.3 4.9 %collective-permute-start = (f32[1,1,3,3,4,360]{5,4,3,2,1,0:T(4,128)S(1)}, f32[1,1,3,3,4,360]{5,4,3,2,1,0:T(4,128)S(1)}, u32[]{:S(2)}, u32[]{:S(2)}) collective-permute-start(f32[1,1,3,3,4,360]{5,4,3,2,1,0:T(4,128)S(1)} %maximum_bitcast_fusion.1), channel_id=1, source_target_pairs={{0,4},{4,8},{8,12},{12,16},{16,20},{20,24},{24,28},{28,32},{32,36}... | collective-permute-start | bytes 155528 | tf_op jit(solution)/shard_map/ppermute | solution.py:31
  10.2 13.0 %collective-permute-start.1 = (f32[1,1,3,3,4,360]{5,4,3,2,1,0:T(4,128)S(1)}, f32[1,1,3,3,4,360]{5,4,3,2,1,0:T(4,128)S(1)}, u32[]{:S(2)}, u32[]{:S(2)}) collective-permute-start(f32[1,1,3,3,4,360]{5,4,3,2,1,0:T(4,128)S(1)} %maximum_bitcast_fusion.1), channel_id=1, source_target_pairs={{4,0},{8,4},{12,8},{16,12},{20,16},{24,20},{28,24},{32,28},{36,32}... | collective-permute-start | bytes 155528 | tf_op jit(solution)/shard_map/ppermute | solution.py:32
  23.3 2.1 fusion.32
  27.3 2.1 fusion.31
  33.1 4.8 %collective-permute-start.3 = (f32[3,1,3,3,4,360]{5,4,3,2,1,0:T(4,128)S(1)}, f32[3,1,3,3,4,360]{5,4,3,2,1,0:T(4,128)S(1)}, u32[]{:S(2)}, u32[]{:S(2)}) collective-permute-start(f32[3,1,3,3,4,360]{5,4,3,2,1,0:T(4,128)S(1)} %pad_maximum_fusion.1), channel_id=1, source_target_pairs={{1,0},{2,1},{3,2},{0,3},{5,4},{6,5},{7,6},{4,7},{9,8},{10,9},{11,1... | collective-permute-start | bytes 466568 | tf_op jit(solution)/shard_map/ppermute | solution.py:32
  42.3 2.6 reshape.190
  45.4 2.5 reshape.191
  48.1 2.5 reshape.192
  50.8 2.5 reshape.193
  53.3 7.1 %fusion.4 = (f32[1,1,3,3,4,8100]{5,4,3,2,1,0:T(4,128)}, f32[3,3,4,8100]{3,2,1,0:T(4,128)S(1)}, f32[3,3,4,8100]{3,2,1,0:T(4,128)S(1)}, f32[3,3,4,8100]{3,2,1,0:T(4,128)S(1)}, f32[3,3,4,8100]{3,2,1,0:T(4,128)S(1)}) fusion(f32[3,3,1,8100]{3,2,1,0:T(1,128)} %get-tuple-element.76, f32[3,3,3,8100]{3,2,1,0:T(4,128)} %get-tuple-element.78, ...), kind=kLoop, calls=%fused_computation.8 | loop fusion | flops 5832000 | bytes 18765856 | tf_op jit(solution)/shard_map/broadcast_in_dim | solution.py:188
  63.8 9.6 %collective-permute-start.5 = (f32[1,1,3,360]{3,2,1,0:T(4,128)S(1)}, f32[1,1,3,360]{3,2,1,0:T(4,128)S(1)}, u32[]{:S(2)}, u32[]{:S(2)}) collective-permute-start(f32[1,1,3,360]{3,2,1,0:T(4,128)S(1)} %maximum_bitcast_fusion.2), channel_id=1, source_target_pairs={{4,0},{8,4},{12,8},{16,12},{20,16},{24,20},{28,24},{32,28},{36,32}... | collective-permute-start | bytes 12968 | tf_op jit(solution)/shard_map/ppermute | solution.py:32
  74.3 3.3 %collective-permute-start.6 = (f32[3,1,3,360]{3,2,1,0:T(4,128)S(1)}, f32[3,1,3,360]{3,2,1,0:T(4,128)S(1)}, u32[]{:S(2)}, u32[]{:S(2)}) collective-permute-start(f32[3,1,3,360]{3,2,1,0:T(4,128)S(1)} %pad_maximum_fusion.4), channel_id=1, source_target_pairs={{0,1},{1,2},{2,3},{3,0},{4,5},{5,6},{6,7},{7,4},{8,9},{9,10},{10,1... | collective-permute-start | bytes 38888 | tf_op jit(solution)/shard_map/ppermute | solution.py:31
  77.6 3.5 %collective-permute-start.7 = (f32[3,1,3,360]{3,2,1,0:T(4,128)S(1)}, f32[3,1,3,360]{3,2,1,0:T(4,128)S(1)}, u32[]{:S(2)}, u32[]{:S(2)}) collective-permute-start(f32[3,1,3,360]{3,2,1,0:T(4,128)S(1)} %pad_maximum_fusion.4), channel_id=1, source_target_pairs={{1,0},{2,1},{3,2},{0,3},{5,4},{6,5},{7,6},{4,7},{9,8},{10,9},{11,1... | collective-permute-start | bytes 38888 | tf_op jit(solution)/shard_map/ppermute | solution.py:32
  85.1 7.1 %all-reduce.17 = (f32[]{:T(128)}, f32[]{:T(128)}) all-reduce(f32[]{:T(128)} %get-tuple-element.42, f32[]{:T(128)} %get-tuple-element.41), channel_id=1, replica_groups=mesh['tiles_0'=4,'tiles_1'=32,'tiles_2'=2,'strip'=4] {'tiles_0'}, use_global_device_ids=true, to_apply=%region_2.6 | all-reduce | flops 2 | bytes 16 | tf_op jit(solution)/shard_map/psum | solution.py:20
  92.3 49.7 %all-reduce.13 = (f32[]{:T(128)}, f32[]{:T(128)}) all-reduce(f32[]{:T(128)} %get-tuple-element.56, f32[]{:T(128)} %get-tuple-element.57), channel_id=1, replica_groups=mesh['tiles_0'=4,'tiles_1'=32,'tiles_2'=2,'strip'=4] {'tiles_1'}, use_global_device_ids=true, to_apply=%region_3.7 | all-reduce | flops 2 | bytes 16 | tf_op jit(solution)/shard_map/psum | solution.py:20
  142.0 14.9 %all-reduce.19 = (f32[]{:T(128)}, f32[]{:T(128)}) all-reduce(f32[]{:T(128)} %get-tuple-element.48, f32[]{:T(128)} %get-tuple-element.49), channel_id=1, replica_groups=mesh['tiles_0'=4,'tiles_1'=32,'tiles_2'=2,'strip'=4] {'tiles_2'}, use_global_device_ids=true, to_apply=%region_4.8 | all-reduce | flops 2 | bytes 16 | tf_op jit(solution)/shard_map/psum | solution.py:20
  156.9 9.2 %all-reduce.15 = (f32[]{:T(128)}, f32[]{:T(128)}) all-reduce(f32[]{:T(128)} %get-tuple-element.60, f32[]{:T(128)} %get-tuple-element.61), channel_id=1, replica_groups=mesh['tiles_0'=4,'tiles_1'=32,'tiles_2'=2,'strip'=4] {'strip'}, use_global_device_ids=true, to_apply=%region_5.9 | all-reduce | flops 2 | bytes 16 | tf_op jit(solution)/shard_map/psum | solution.py:20
  168.0 5.6 %collective-permute-start.8 = (f32[1,1,3,360]{3,2,1,0:T(4,128)S(1)}, f32[1,1,3,360]{3,2,1,0:T(4,128)S(1)}, u32[]{:S(2)}, u32[]{:S(2)}) collective-permute-start(f32[1,1,3,360]{3,2,1,0:T(4,128)S(1)} %maximum_bitcast_fusion.3), channel_id=1, source_target_pairs={{0,4},{4,8},{8,12},{12,16},{16,20},{20,24},{24,28},{28,32},{32,36}... | collective-permute-start | bytes 12968 | tf_op jit(solution)/shard_map/ppermute | solution.py:31
  175.7 2.9 %collective-permute-done.9 = f32[1,1,3,360]{3,2,1,0:T(4,128)S(1)} collective-permute-done((f32[1,1,3,360]{3,2,1,0:T(4,128)S(1)}, f32[1,1,3,360]{3,2,1,0:T(4,128)S(1)}, u32[]{:S(2)}, u32[]{:S(2)}) %collective-permute-start.9) | collective-permute-done | bytes 4352 | tf_op jit(solution)/shard_map/ppermute | solution.py:32
  180.5 4.6 %collective-permute-start.11 = (f32[3,1,3,360]{3,2,1,0:T(4,128)S(1)}, f32[3,1,3,360]{3,2,1,0:T(4,128)S(1)}, u32[]{:S(2)}, u32[]{:S(2)}) collective-permute-start(f32[3,1,3,360]{3,2,1,0:T(4,128)S(1)} %pad_maximum_fusion.5), channel_id=1, source_target_pairs={{1,0},{2,1},{3,2},{0,3},{5,4},{6,5},{7,6},{4,7},{9,8},{10,9},{11,1... | collective-permute-start | bytes 38888 | tf_op jit(solution)/shard_map/ppermute | solution.py:32
  189.0 8.4 %all-reduce.16 = (f32[]{:T(128)}, f32[]{:T(128)}) all-reduce(f32[]{:T(128)} %get-tuple-element.40, f32[]{:T(128)} %get-tuple-element.39), channel_id=1, replica_groups=mesh['tiles_0'=4,'tiles_1'=32,'tiles_2'=2,'strip'=4] {'tiles_0'}, use_global_device_ids=true, to_apply=%region_12.16 | all-reduce | flops 2 | bytes 16 | tf_op jit(solution)/shard_map/psum | solution.py:20
  197.4 44.6 %all-reduce.12 = (f32[]{:T(128)}, f32[]{:T(128)}) all-reduce(f32[]{:T(128)} %get-tuple-element.54, f32[]{:T(128)} %get-tuple-element.55), channel_id=1, replica_groups=mesh['tiles_0'=4,'tiles_1'=32,'tiles_2'=2,'strip'=4] {'tiles_1'}, use_global_device_ids=true, to_apply=%region_13.17 | all-reduce | flops 2 | bytes 16 | tf_op jit(solution)/shard_map/psum | solution.py:20
  242.0 15.2 %all-reduce.18 = (f32[]{:T(128)}, f32[]{:T(128)}) all-reduce(f32[]{:T(128)} %get-tuple-element.46, f32[]{:T(128)} %get-tuple-element.47), channel_id=1, replica_groups=mesh['tiles_0'=4,'tiles_1'=32,'tiles_2'=2,'strip'=4] {'tiles_2'}, use_global_device_ids=true, to_apply=%region_14.18 | all-reduce | flops 2 | bytes 16 | tf_op jit(solution)/shard_map/psum | solution.py:20
  257.2 9.9 %all-reduce.14 = (f32[]{:T(128)}, f32[]{:T(128)}) all-reduce(f32[]{:T(128)} %get-tuple-element.58, f32[]{:T(128)} %get-tuple-element.59), channel_id=1, replica_groups=mesh['tiles_0'=4,'tiles_1'=32,'tiles_2'=2,'strip'=4] {'strip'}, use_global_device_ids=true, to_apply=%region_15.19 | all-reduce | flops 2 | bytes 16 | tf_op jit(solution)/shard_map/psum | solution.py:20
  (125 shorter events, 33.3 us)
Async XLA Ops:
  5.3 25.8 %collective-permute-start = (f32[1,1,3,3,4,360]{5,4,3,2,1,0:T(4,128)S(1)}, f32[1,1,3,3,4,360]{5,4,3,2,1,0:T(4,128)S(1)}, u32[]{:S(2)}, u32[]{:S(2)}) collective-permute-start(f32[1,1,3,3,4,360]{5,4,3,2,1,0:T(4,128)S(1)} %maximum_bitcast_fusion.1), channel_id=1, source_target_pairs={{0,4},{4,8},{8,12},{12,16},{16,20},{20,24},{24,28},{28,32},{32,36}... | collective-permute-start | bytes 155528 | tf_op jit(solution)/shard_map/ppermute | solution.py:31
  10.2 20.9 %collective-permute-start.1 = (f32[1,1,3,3,4,360]{5,4,3,2,1,0:T(4,128)S(1)}, f32[1,1,3,3,4,360]{5,4,3,2,1,0:T(4,128)S(1)}, u32[]{:S(2)}, u32[]{:S(2)}) collective-permute-start(f32[1,1,3,3,4,360]{5,4,3,2,1,0:T(4,128)S(1)} %maximum_bitcast_fusion.1), channel_id=1, source_target_pairs={{4,0},{8,4},{12,8},{16,12},{20,16},{24,20},{28,24},{32,28},{36,32}... | collective-permute-start | bytes 155528 | tf_op jit(solution)/shard_map/ppermute | solution.py:32
  29.4 1.3 copy-start.7
  29.4 1.3 copy-start.3
  29.5 1.4 copy-start.6
  31.1 7.3 %collective-permute-start.2 = (f32[3,1,3,3,4,360]{5,4,3,2,1,0:T(4,128)S(1)}, f32[3,1,3,3,4,360]{5,4,3,2,1,0:T(4,128)S(1)}, u32[]{:S(2)}, u32[]{:S(2)}) collective-permute-start(f32[3,1,3,3,4,360]{5,4,3,2,1,0:T(4,128)S(1)} %pad_maximum_fusion.1), channel_id=1, source_target_pairs={{0,1},{1,2},{2,3},{3,0},{4,5},{5,6},{6,7},{7,4},{8,9},{9,10},{10,1... | collective-permute-start | bytes 466568 | tf_op jit(solution)/shard_map/ppermute | solution.py:31
  33.1 6.8 %collective-permute-start.3 = (f32[3,1,3,3,4,360]{5,4,3,2,1,0:T(4,128)S(1)}, f32[3,1,3,3,4,360]{5,4,3,2,1,0:T(4,128)S(1)}, u32[]{:S(2)}, u32[]{:S(2)}) collective-permute-start(f32[3,1,3,3,4,360]{5,4,3,2,1,0:T(4,128)S(1)} %pad_maximum_fusion.1), channel_id=1, source_target_pairs={{1,0},{2,1},{3,2},{0,3},{5,4},{6,5},{7,6},{4,7},{9,8},{10,9},{11,1... | collective-permute-start | bytes 466568 | tf_op jit(solution)/shard_map/ppermute | solution.py:32
  50.7 2.6 copy-start
  50.7 2.6 copy-start.4
  50.7 2.5 copy-start.5
  60.4 0.9 copy-start.1
  61.9 11.7 %collective-permute-start.4 = (f32[1,1,3,360]{3,2,1,0:T(4,128)S(1)}, f32[1,1,3,360]{3,2,1,0:T(4,128)S(1)}, u32[]{:S(2)}, u32[]{:S(2)}) collective-permute-start(f32[1,1,3,360]{3,2,1,0:T(4,128)S(1)} %maximum_bitcast_fusion.2), channel_id=1, source_target_pairs={{0,4},{4,8},{8,12},{12,16},{16,20},{20,24},{24,28},{28,32},{32,36}... | collective-permute-start | bytes 12968 | tf_op jit(solution)/shard_map/ppermute | solution.py:31
  63.8 10.5 %collective-permute-start.5 = (f32[1,1,3,360]{3,2,1,0:T(4,128)S(1)}, f32[1,1,3,360]{3,2,1,0:T(4,128)S(1)}, u32[]{:S(2)}, u32[]{:S(2)}) collective-permute-start(f32[1,1,3,360]{3,2,1,0:T(4,128)S(1)} %maximum_bitcast_fusion.2), channel_id=1, source_target_pairs={{4,0},{8,4},{12,8},{16,12},{20,16},{24,20},{28,24},{32,28},{36,32}... | collective-permute-start | bytes 12968 | tf_op jit(solution)/shard_map/ppermute | solution.py:32
  74.3 9.9 %copy-start.2 = (f32[1,1,3,8100]{3,1,2,0:T(1,128)S(1)}, f32[1,1,3,8100]{3,1,2,0:T(1,128)}, u32[]{:S(2)}) copy-start(f32[1,1,3,8100]{3,1,2,0:T(1,128)} %param.17) | copy-start | bytes 291604
  74.3 7.0 %collective-permute-start.6 = (f32[3,1,3,360]{3,2,1,0:T(4,128)S(1)}, f32[3,1,3,360]{3,2,1,0:T(4,128)S(1)}, u32[]{:S(2)}, u32[]{:S(2)}) collective-permute-start(f32[3,1,3,360]{3,2,1,0:T(4,128)S(1)} %pad_maximum_fusion.4), channel_id=1, source_target_pairs={{0,1},{1,2},{2,3},{3,0},{4,5},{5,6},{6,7},{7,4},{8,9},{9,10},{10,1... | collective-permute-start | bytes 38888 | tf_op jit(solution)/shard_map/ppermute | solution.py:31
  77.6 4.5 %collective-permute-start.7 = (f32[3,1,3,360]{3,2,1,0:T(4,128)S(1)}, f32[3,1,3,360]{3,2,1,0:T(4,128)S(1)}, u32[]{:S(2)}, u32[]{:S(2)}) collective-permute-start(f32[3,1,3,360]{3,2,1,0:T(4,128)S(1)} %pad_maximum_fusion.4), channel_id=1, source_target_pairs={{1,0},{2,1},{3,2},{0,3},{5,4},{6,5},{7,6},{4,7},{9,8},{10,9},{11,1... | collective-permute-start | bytes 38888 | tf_op jit(solution)/shard_map/ppermute | solution.py:32
  168.0 7.7 %collective-permute-start.8 = (f32[1,1,3,360]{3,2,1,0:T(4,128)S(1)}, f32[1,1,3,360]{3,2,1,0:T(4,128)S(1)}, u32[]{:S(2)}, u32[]{:S(2)}) collective-permute-start(f32[1,1,3,360]{3,2,1,0:T(4,128)S(1)} %maximum_bitcast_fusion.3), channel_id=1, source_target_pairs={{0,4},{4,8},{8,12},{12,16},{16,20},{20,24},{24,28},{28,32},{32,36}... | collective-permute-start | bytes 12968 | tf_op jit(solution)/shard_map/ppermute | solution.py:31
  173.6 4.9 %collective-permute-start.9 = (f32[1,1,3,360]{3,2,1,0:T(4,128)S(1)}, f32[1,1,3,360]{3,2,1,0:T(4,128)S(1)}, u32[]{:S(2)}, u32[]{:S(2)}) collective-permute-start(f32[1,1,3,360]{3,2,1,0:T(4,128)S(1)} %maximum_bitcast_fusion.3), channel_id=1, source_target_pairs={{4,0},{8,4},{12,8},{16,12},{20,16},{24,20},{28,24},{32,28},{36,32}... | collective-permute-start | bytes 12968 | tf_op jit(solution)/shard_map/ppermute | solution.py:32
  178.6 6.6 %collective-permute-start.10 = (f32[3,1,3,360]{3,2,1,0:T(4,128)S(1)}, f32[3,1,3,360]{3,2,1,0:T(4,128)S(1)}, u32[]{:S(2)}, u32[]{:S(2)}) collective-permute-start(f32[3,1,3,360]{3,2,1,0:T(4,128)S(1)} %pad_maximum_fusion.5), channel_id=1, source_target_pairs={{0,1},{1,2},{2,3},{3,0},{4,5},{5,6},{6,7},{7,4},{8,9},{9,10},{10,1... | collective-permute-start | bytes 38888 | tf_op jit(solution)/shard_map/ppermute | solution.py:31
  180.5 5.4 %collective-permute-start.11 = (f32[3,1,3,360]{3,2,1,0:T(4,128)S(1)}, f32[3,1,3,360]{3,2,1,0:T(4,128)S(1)}, u32[]{:S(2)}, u32[]{:S(2)}) collective-permute-start(f32[3,1,3,360]{3,2,1,0:T(4,128)S(1)} %pad_maximum_fusion.5), channel_id=1, source_target_pairs={{1,0},{2,1},{3,2},{0,3},{5,4},{6,5},{7,6},{4,7},{9,8},{10,9},{11,1... | collective-permute-start | bytes 38888 | tf_op jit(solution)/shard_map/ppermute | solution.py:32
where the time goes:
time: 275 us; the launch traced here: 273 us
  blocking collectives  159 us (58%)
  starting transfers between devices  57 us (21%)
  local copies, waits for them, and re-layouts  29.5 us (11%)
  other arithmetic  13.7 us (5%)
  between operations  7.13 us (3%)
  waiting for transfers between devices  6.72 us (2%)
    psum x8, blocking collectives, over_axes(): value = lax.psum(value, axis)  159 us
    ppermute x6, starting transfers between devices, extended(): after = lax.ppermute(leading, axis, down)  37.4 us
    ppermute x6, starting transfers between devices, extended(): before = lax.ppermute(last, axis, up)  19.6 us
    broadcast_in_dim x1, other arithmetic, on_device(): return (updated[None, None], solution[None, None], residual[None, None])  7.07 us
    ppermute x6, waiting for transfers between devices, extended(): after = lax.ppermute(leading, axis, down)  6.58 us
  transfers between devices with their start and end apart: 12, of which 6 were waited for; matrix products, arithmetic and copies ran while one was open for 3% of the time, Pallas kernels for 0%

commit v1 on v0

v1 whole, which is shorter than its diff:
```python
import functools

import jax
import jax.numpy as jnp
from jax import lax
from jax.experimental import pallas as pl
from jax.experimental.pallas import tpu as pltpu
from jax.sharding import PartitionSpec as P

TILE = 90
SLOTS = 3
FIELDS = 3
LEVELS = 4
CELLS = TILE * TILE
LANES = 128
BLOCKS = 64
WIDE = LANES * BLOCKS
SPLIT = 45
CENTRE = 5.0
MESH = pl.DeviceIdType.MESH
WEST, EAST, SOUTH, NORTH = 0, 1, 2, 3


def take_lanes(rows, index):
    return jnp.take_along_axis(rows, index, axis=1, mode="promise_in_bounds")


def block(k):
    return slice(k * LANES, (k + 1) * LANES)


def beside(x, not_west, not_east):
    west = pltpu.roll(x, 1, 1) * not_west
    east = pltpu.roll(x, WIDE - 1, 1) * not_east
    south = pltpu.roll(x, TILE, 1)
    north = pltpu.roll(x, WIDE - TILE, 1)
    return west, east, south, north


def lane_row(shape=(4, LANES)):
    return lax.broadcasted_iota(jnp.int32, shape, 1)


def rims_of(load, rim):
    def merged(first, last):
        values = [(load(k), rim(k)) for k in range(first, last)]
        chains = []
        for start in range(4):
            total = None
            for value, mask in values[start::4]:
                kept = value * mask
                total = kept if total is None else total + kept
            chains.append(total)
        return (chains[0] + chains[1]) + (chains[2] + chains[3])

    low = merged(0, SPLIT)
    high = merged(SPLIT, BLOCKS)
    lane = lane_row()
    west_lane = (lane * TILE) & (LANES - 1)
    east_lane = (lane * TILE + (TILE - 1)) & (LANES - 1)
    west = jnp.where(lane < 64, take_lanes(low, west_lane), take_lanes(high, west_lane))
    east = jnp.where(lane < 64, take_lanes(low, east_lane), take_lanes(high, east_lane))
    south = load(0)
    north = jnp.where(lane < 54, pltpu.roll(load(62), 54, 1), pltpu.roll(load(63), 54, 1))
    return west, east, south, north


def spread_rims(west, east, south, north):
    lane = lane_row()
    half = lax.shift_right_logical(lane, 1)
    odd = (lane & 1) == 1
    west_row = (half * 37) & 63
    east_row = (lax.shift_right_logical(lane + 39, 1) * 37) & 63
    low = jnp.where(odd, take_lanes(east, east_row), take_lanes(west, west_row))
    high = jnp.where(odd, take_lanes(east, east_row + 64), take_lanes(west, west_row + 64))
    first = jnp.where(lane < TILE, south, 0.0)
    turned = pltpu.roll(north, 74, 1)
    before = jnp.where(lane >= 74, turned, 0.0)
    final = jnp.where(lane < 36, turned, 0.0)
    columns = jnp.concatenate([low] * SPLIT + [high] * (BLOCKS - SPLIT), axis=1)
    return columns, first, before, final


def flip(rows, flags):
    back = (TILE - 1 - lane_row()) & (LANES - 1)
    return jnp.where(flags > 0.0, take_lanes(rows, back), rows)


def kernel(
    sizes,
    links, spread, mixing, thickness, fields, wet_land, diagonal,
    adjoint, answer, remainder,
    raw, raw_wet, raw_diagonal, masked, stepped, wet, wet_levels, centre_term,
    not_west, not_east, rim_mask, east_flow, north_flow, first_field, second_field, third_field,
    flags, turn_a, turn_b, valid, spreads, mixings, weights,
    rows_a, rows_b, slab_rows, answer_rows, remainder_rows,
    send_1, recv_1, send_2, recv_2, send_3, recv_3, send_slab, recv_slab,
    plane, column,
    in_sems, out_sem, send_sems, recv_sems, hello,
):
    groups, strips, length = sizes
    t = lax.axis_index("tiles")
    s = lax.axis_index("strip")
    core = lax.rem(t, 2)
    chip = lax.div(t, 2)
    z = lax.rem(chip, length)
    x = lax.div(chip, length)
    planes = groups // length * strips
    here = (x * strips + s) * 2 + core

    def beside_device(dt, ds):
        return (lax.rem(t + dt + groups, groups), lax.rem(s + ds + strips, strips))

    def plane_device(offset):
        other = lax.rem(here + offset, planes)
        at_x = lax.div(other, 2 * strips)
        at_s = lax.rem(lax.div(other, 2), strips)
        return ((at_x * length + z) * 2 + lax.rem(other, 2), at_s)

    def column_device(offset):
        return ((x * length + lax.rem(z + offset + length, length)) * 2 + core, s)

    reach = min(4, length // 2)
    near = [(dt, ds) for dt in (-1, 0, 1) for ds in (-1, 0, 1) if (dt, ds) != (0, 0)]
    along = []
    for d in range(1, reach + 1):
        along += [d] if 2 * d == length else [d, -d]
    barrier = pltpu.get_barrier_semaphore()
    for dt, ds in near:
        pl.semaphore_signal(barrier, inc=1, device_id=beside_device(dt, ds), device_id_type=MESH)
    for offset in along:
        pl.semaphore_signal(barrier, inc=1, device_id=column_device(offset), device_id_type=MESH)
    for offset in range(1, planes):
        pl.semaphore_signal(barrier, inc=1, device_id=plane_device(offset), device_id_type=MESH)

    wet_copy = pltpu.make_async_copy(wet_land, raw_wet, in_sems.at[9])
    wet_copy.start()
    field_copies = {}
    for f in (0, 1, 2):
        for k in range(SLOTS):
            a = k * FIELDS + f
            field_copies[a] = pltpu.make_async_copy(fields.at[a], raw.at[a], in_sems.at[a])
            field_copies[a].start()
    diagonal_copy = pltpu.make_async_copy(diagonal, raw_diagonal, in_sems.at[10])
    diagonal_copy.start()

    cell = lax.broadcasted_iota(jnp.int32, (4, WIDE), 1)
    row = lax.shift_right_logical(cell * 11651, 20)
    place = cell - row * TILE
    not_west[...] = jnp.where(place == 0, 0.0, 1.0)
    not_east[...] = jnp.where(place == TILE - 1, 0.0, 1.0)
    at_rim = (place == 0) | (place == TILE - 1)
    rim_mask[...] = jnp.where(at_rim & (cell < CELLS), 1.0, 0.0)
    zero_row = jnp.zeros((1, LANES), jnp.float32)
    for side in range(4):
        for k in range(SLOTS):
            code = links[k, side, 3]
            there = (links[k, side, 2] >= 0).astype(jnp.float32)
            one = lambda flag: flag.astype(jnp.float32)
            fill = lambda value: jnp.full((1, LANES), value, jnp.float32)
            flags[side, k : k + 1, :] = fill(one(code != 0))
            valid[side, k : k + 1, :] = fill(there)
            turn_a[side, k : k + 1, :] = fill(there * (one(code == 0) - one(code == 2)))
            turn_b[side, k : k + 1, :] = fill(there * (one(code == 1) - one(code == 3)))
        for table in (flags, valid, turn_a, turn_b, rows_a, rows_b):
            table[side, 3:4, :] = zero_row
    for l in range(LEVELS):
        weights[l : l + 1, :] = jnp.full((1, LANES), thickness[l], jnp.float32)
        mixings[l : l + 1, :] = jnp.full((1, LANES), mixing[l], jnp.float32)
        for f in range(FIELDS):
            spreads[f, l : l + 1, :] = jnp.full((1, LANES), spread[f, l], jnp.float32)
    for table in (wet, centre_term, east_flow, north_flow):
        table[...] = jnp.zeros((4, WIDE), jnp.float32)
    tail = jnp.zeros((4, LANES), jnp.float32)
    for a in range(SLOTS * FIELDS):
        masked[a, :, block(63)] = tail

    def tiled(rows):
        return jnp.concatenate([rows] * BLOCKS, axis=1)

    wet_copy.wait()
    wet[0:3, 0:CELLS] = raw_wet[...].astype(jnp.float32)
    for k in range(SLOTS):
        wet_levels[k] = jnp.broadcast_to(wet[k : k + 1, :], (4, WIDE))

    def mask_field(a, k):
        kept = wet_levels[k, :, 0:CELLS] > 0.0
        masked[a, :, 0:CELLS] = jnp.where(kept, raw[a], 0.0)

    for k in range(SLOTS):
        for f, flow in ((0, east_flow), (1, north_flow)):
            a = k * FIELDS + f
            field_copies[a].wait()
            mask_field(a, k)
            scaled = masked[a] * tiled(weights[...])
            flow[k : k + 1, :] = jnp.sum(scaled, axis=0, keepdims=True)

    rim = lambda k: rim_mask[:, block(k)]
    for part, flow in ((0, east_flow), (1, north_flow)):
        for side, value in enumerate(rims_of(lambda k: flow[:, block(k)], rim)):
            for k in range(SLOTS):
                send_1[side, k, part : part + 1, :] = value[k : k + 1, :]

    pl.semaphore_wait(barrier, len(near) + len(along) + planes - 1)

    def exchange(sent, received, slot, width):
        for d in (-1, 0, 1):
            for side, device in (
                (EAST, beside_device(1, d)),
                (WEST, beside_device(-1, d)),
                (NORTH, beside_device(d, 1)),
                (SOUTH, beside_device(d, -1)),
            ):
                pltpu.make_async_remote_copy(
                    src_ref=sent.at[side],
                    dst_ref=received.at[side ^ 1, pl.ds((1 - d) * width, width)],
                    send_sem=send_sems.at[slot],
                    recv_sem=recv_sems.at[slot],
                    device_id=device,
                    device_id_type=MESH,
                ).start()

    def whole(buffer, slot):
        return pltpu.make_async_remote_copy(
            src_ref=buffer,
            dst_ref=buffer,
            send_sem=send_sems.at[slot],
            recv_sem=recv_sems.at[slot],
            device_id=beside_device(1, 0),
            device_id_type=MESH,
        )

    def source_of(k, side):
        step = links[k, side, 1] if side in (WEST, EAST) else links[k, side, 0]
        step = jnp.clip(step, -1, 1) + 1
        return step * SLOTS + jnp.clip(links[k, side, 2], 0, SLOTS - 1)

    exchange(send_1, recv_1, 0, SLOTS)
    greeting = reach
    rounds = []
    while greeting < length // 2:
        rounds.append(greeting)
        greeting *= 2

    def greet(i):
        if i < len(rounds):
            for offset in (rounds[i], -rounds[i]):
                pl.semaphore_signal(
                    hello.at[i], inc=1, device_id=column_device(offset), device_id_type=MESH
                )

    def greeted(i):
        if i < len(rounds):
            pl.semaphore_wait(hello.at[i], 2)

    greet(0)

    for k in range(SLOTS):
        field_copies[k * FIELDS + 2].wait()
        mask_field(k * FIELDS + 2, k)

    def slab_rims(a, carry):
        for side, value in enumerate(rims_of(lambda k: masked[a, :, block(k)], rim)):
            send_slab[side, a] = value
        return carry

    lax.fori_loop(0, SLOTS * FIELDS, slab_rims, 0)
    exchange(send_slab, recv_slab, 3, SLOTS * FIELDS)

    def flux_inside():
        west, east, _, _ = beside(east_flow[...], not_west[...], not_east[...])
        _, _, south, north = beside(north_flow[...], not_west[...], not_east[...])
        return 0.5 * wet[...] * (east - west + north - south)

    first_field[...] = flux_inside()
    diagonal_copy.wait()
    centre_term[0:3, 0:CELLS] = raw_diagonal[...] + (4.0 - CENTRE)

    def add_rims(target, scale, west, east, south, north):
        columns, first, before, final = spread_rims(west, east, south, north)
        target[...] += scale * wet[...] * (columns * rim_mask[...])
        for k, value in ((0, first), (62, before), (63, final)):
            target[:, block(k)] += scale * wet[:, block(k)] * value

    def operator_inside(target, values):
        west, east, south, north = beside(values[...], not_west[...], not_east[...])
        target[...] = wet[...] * (
            centre_term[...] * values[...] - ((west + east) + (south + north))
        )

    def send_surface(values, sent, received, slot):
        for side, value in enumerate(rims_of(lambda k: values[:, block(k)], rim)):
            for k in range(SLOTS):
                sent[side, k] = value[k : k + 1, :]
        exchange(sent, received, slot, SLOTS)

    def received_surface(received, slot):
        whole(received, slot).wait_recv()
        out = []
        for side in range(4):
            for k in range(SLOTS):
                rows_a[side, k : k + 1, :] = received[side, source_of(k, side)]
            out.append(flip(rows_a[side] * valid[side], flags[side]))
        return out

    whole(recv_1, 0).wait_recv()
    gathered = []
    for side in range(4):
        for k in range(SLOTS):
            pair = recv_1[side, source_of(k, side)]
            rows_a[side, k : k + 1, :] = pair[0:1, :]
            rows_b[side, k : k + 1, :] = pair[1:2, :]
        a, b = turn_a[side], turn_b[side]
        if side in (WEST, EAST):
            turned = a * rows_a[side] + b * rows_b[side]
        else:
            turned = a * rows_b[side] - b * rows_a[side]
        if side in (WEST, SOUTH):
            turned = -turned
        gathered.append(flip(turned, flags[side]))
    add_rims(first_field, 0.5, *gathered)
    send_surface(first_field, send_2, recv_2, 1)

    operator_inside(second_field, first_field)
    add_rims(second_field, -1.0, *received_surface(recv_2, 1))
    send_surface(second_field, send_3, recv_3, 2)
    greeted(0)
    greet(1)

    operator_inside(third_field, second_field)

    def total(value):
        return jnp.sum(jnp.sum(value, axis=1, keepdims=True), axis=0, keepdims=True)

    moment_0 = total(first_field[...] * first_field[...])
    moment_1 = total(first_field[...] * second_field[...])
    moment_2 = total(second_field[...] * second_field[...])
    add_rims(third_field, -1.0, *received_surface(recv_3, 2))
    moment_3 = total(second_field[...] * third_field[...])
    lane = lane_row((1, LANES))
    packed = jnp.where(lane == 0, moment_0, 0.0)
    packed = jnp.where(lane == 1, moment_1, packed)
    packed = jnp.where(lane == 2, moment_2, packed)
    packed = jnp.where(lane == 3, moment_3, packed)

    def share(buffer, position, value, devices, slot):
        buffer[position] = value
        for device in devices:
            pltpu.make_async_remote_copy(
                src_ref=buffer.at[position],
                dst_ref=buffer.at[position],
                send_sem=send_sems.at[slot],
                recv_sem=recv_sems.at[slot],
                device_id=device,
                device_id_type=MESH,
            ).start()

    def shared(buffer, count, slot):
        return whole(buffer.at[pl.ds(0, count)], slot)

    share(plane, here, packed, [plane_device(o) for o in range(1, planes)], 4)
    for i in range(1, len(rounds)):
        greeted(i)
        greet(i + 1)
    shared(plane, planes - 1, 4).wait_recv()
    packed = jnp.sum(plane[...], axis=0)
    offsets = []
    for d in range(length // 2, 0, -1):
        offsets += [d] if 2 * d == length else [d, -d]
    share(column, z, packed, [column_device(o) for o in offsets], 5)

    whole(recv_slab, 3).wait_recv()

    def slab_orient(k, carry):
        for side in range(4):
            code = links[k, side, 3]
            there = (links[k, side, 2] >= 0).astype(jnp.float32)
            cosine = there * ((code == 0).astype(jnp.float32) - (code == 2).astype(jnp.float32))
            sine = there * ((code == 1).astype(jnp.float32) - (code == 3).astype(jnp.float32))
            turn = (code != 0).astype(jnp.float32)
            at = source_of(k, side) * FIELDS
            u, v, scalar = (recv_slab[side, at + f] for f in range(FIELDS))
            values = (cosine * u + sine * v, cosine * v - sine * u, there * scalar)
            for f in range(FIELDS):
                slab_rows[side, k * FIELDS + f] = flip(
                    values[f], jnp.full((4, LANES), turn, jnp.float32)
                )
        return carry

    lax.fori_loop(0, SLOTS, slab_orient, 0)

    def slab_step(a, carry):
        k = lax.div(a, FIELDS)
        f = lax.rem(a, FIELDS)
        m = masked[a]
        west, east, south, north = beside(m, not_west[...], not_east[...])
        columns, first, before, final = spread_rims(*(slab_rows[side, a] for side in range(4)))
        flat = (west + east) + (south + north) + columns * rim_mask[...]
        flat = jnp.concatenate(
            [
                flat[:, block(0)] + first,
                flat[:, LANES : 62 * LANES],
                flat[:, block(62)] + before,
                flat[:, block(63)] + final,
            ],
            axis=1,
        )
        flat = flat - 4.0 * m
        above = jnp.concatenate([m[1:4], m[3:4]], axis=0)
        below = jnp.concatenate([m[0:1], m[0:3]], axis=0)
        vertical = above + below - 2.0 * m
        updated = wet_levels[k] * (
            m + tiled(spreads[f]) * flat + tiled(mixings[...]) * vertical
        )
        stepped[a] = updated[:, 0:CELLS]
        pltpu.make_async_copy(stepped.at[a], adjoint.at[a], out_sem.at[0]).start()
        return carry

    lax.fori_loop(0, SLOTS * FIELDS, slab_step, 0)

    shared(column, length - 1, 5).wait_recv()
    packed = jnp.sum(column[...], axis=0)
    n0, n1, n2, n3 = (
        jnp.sum(jnp.where(lane == i, packed, 0.0), axis=1, keepdims=True) for i in range(4)
    )
    r1, r2, r3 = n1 / n0, n2 / n0, n3 / n0
    mu = r1 + CENTRE
    alpha_0 = 1.0 / mu
    beta = (r2 - r1 * r1) * alpha_0 * alpha_0
    applied = (r1 * r1 * r1 - 2.0 * r1 * r2 + r3) * alpha_0 * alpha_0 + CENTRE * beta
    alpha_1 = beta / (applied - beta * beta * mu)
    c1 = alpha_0 + alpha_1 * (1.0 + beta)
    c2 = alpha_0 * alpha_1
    r, v, w = first_field[...], second_field[...], third_field[...]
    found = (c1 - CENTRE * c2) * r - c2 * v
    left = (1.0 - CENTRE * c1 + CENTRE * CENTRE * c2) * r + (2.0 * CENTRE * c2 - c1) * v + c2 * w
    answer_rows[...] = found[0:3, 0:CELLS]
    remainder_rows[...] = left[0:3, 0:CELLS]
    answer_copy = pltpu.make_async_copy(answer_rows, answer, out_sem.at[1])
    remainder_copy = pltpu.make_async_copy(remainder_rows, remainder, out_sem.at[2])
    answer_copy.start()
    remainder_copy.start()
    for slot, buffer in enumerate((recv_1, recv_2, recv_3, recv_slab)):
        whole(buffer, slot).wait_send()
    shared(plane, planes - 1, 4).wait_send()
    shared(column, length - 1, 5).wait_send()
    pltpu.make_async_copy(stepped, adjoint, out_sem.at[0]).wait()
    answer_copy.wait()
    remainder_copy.wait()


def make(mesh, length):
    groups, strips = mesh.shape["tiles"], mesh.shape["strip"]
    planes = groups // length * strips
    slabs = SLOTS * FIELDS
    f32 = jnp.float32
    V = lambda *shape: pltpu.VMEM(shape, f32)
    smem = pl.BlockSpec(memory_space=pltpu.SMEM)
    hbm = pl.BlockSpec(memory_space=pl.ANY)
    call = pl.pallas_call(
        functools.partial(kernel, (groups, strips, length)),
        out_shape=(
            jax.ShapeDtypeStruct((slabs, LEVELS, CELLS), f32),
            jax.ShapeDtypeStruct((SLOTS, CELLS), f32),
            jax.ShapeDtypeStruct((SLOTS, CELLS), f32),
        ),
        in_specs=[smem] * 4 + [hbm] * 3,
        out_specs=(hbm, hbm, hbm),
        scratch_shapes=[
            V(slabs, LEVELS, CELLS),
            pltpu.VMEM((SLOTS, CELLS), jnp.int32),
            V(SLOTS, CELLS),
            V(slabs, LEVELS, WIDE),
            V(slabs, LEVELS, CELLS),
            V(4, WIDE),
            V(SLOTS, 4, WIDE),
            V(4, WIDE),
            V(4, WIDE), V(4, WIDE), V(4, WIDE),
            V(4, WIDE), V(4, WIDE), V(4, WIDE), V(4, WIDE), V(4, WIDE),
            V(4, 4, LANES), V(4, 4, LANES), V(4, 4, LANES), V(4, 4, LANES),
            V(FIELDS, 4, LANES), V(4, LANES), V(4, LANES),
            V(4, 4, LANES), V(4, 4, LANES), V(4, slabs, 4, LANES),
            V(SLOTS, CELLS), V(SLOTS, CELLS),
            V(4, SLOTS, 2, LANES), V(4, 3 * SLOTS, 2, LANES),
            V(4, SLOTS, 1, LANES), V(4, 3 * SLOTS, 1, LANES),
            V(4, SLOTS, 1, LANES), V(4, 3 * SLOTS, 1, LANES),
            V(4, slabs, 4, LANES), V(4, 3 * slabs, 4, LANES),
            V(planes, 1, LANES), V(length, 1, LANES),
            pltpu.SemaphoreType.DMA((11,)),
            pltpu.SemaphoreType.DMA((3,)),
            pltpu.SemaphoreType.DMA((6,)),
            pltpu.SemaphoreType.DMA((6,)),
            pltpu.SemaphoreType.REGULAR((4,)),
        ],
        compiler_params=pltpu.CompilerParams(
            collective_id=0, has_side_effects=True, vmem_limit_bytes=24 * 1024 * 1024
        ),
        name="slab_and_gradients",
    )

    def on_device(fields, wet_land, links, surface_diagonal, spread, mixing, thickness):
        updated, found, left = call(
            links[0, 0],
            spread,
            mixing,
            thickness,
            fields.reshape(slabs, LEVELS, CELLS),
            wet_land.reshape(SLOTS, CELLS),
            surface_diagonal.reshape(SLOTS, CELLS),
        )
        return updated.reshape(fields.shape), found[None, None], left[None, None]

    return jax.shard_map(
        on_device,
        mesh=mesh,
        in_specs=(
            P("tiles", "strip", None, None, None, None),
            P("tiles", "strip", None, None),
            P("tiles", "strip", None, None, None),
            P("tiles", "strip", None, None),
            P(),
            P(),
            P(),
        ),
        out_specs=(
            P("tiles", "strip", None, None, None, None),
            P("tiles", "strip", None, None),
            P("tiles", "strip", None, None),
        ),
        check_vma=False,
    )


def solution(mesh):
    return make(mesh, 32)
```

time: 275 us -> 62.7 us (0.23)
  blocking collectives: 159 us -> 0 us
  starting transfers between devices: 57 us -> 0 us
  Pallas kernels: 0 us -> 53.3 us
  local copies, waits for them, and re-layouts: 29.5 us -> 8.37 us
  other arithmetic: 13.7 us -> 0 us
  waiting for transfers between devices: 6.72 us -> 0 us
  between operations: 7.13 us -> 0.66 us
    psum x8 -> x0, blocking collectives: 159 us -> none  [over_axes(): value = lax.psum(value, axis)]
    ppermute x12 -> x0, starting transfers between devices: 57 us -> none  [the longest x6 37.4 us: extended(): after = lax.ppermute(leading, axis, down)]
    pallas_call x0 -> x1, Pallas kernels: none -> 53.3 us  [on_device(): call(links[0, 0], spread, mixing, thickness, fields.reshape(slabs, LEVELS...]
    reshape x16 -> x0, local copies, waits for them, and re-layouts: 12.5 us -> none  [the longest x3 2.94 us: beside_values(): jnp.broadcast_to(rims[..., 0, :, None], leading + (width, width))]
    slice x19 -> x0, local copies, waits for them, and re-layouts: 11 us -> none  [the longest x2 3.27 us: slab_step(): below = jnp.concatenate([masked[..., :1, :], masked[..., :-1, :]], axis=-2)]
    unnamed x24 -> x15, local copies, waits for them, and re-layouts: 0.46 us -> 8.37 us
    broadcast_in_dim x4 -> x0, other arithmetic: 7.34 us -> none  [the longest x1 7.07 us: on_device(): return (updated[None, None], solution[None, None], residual[None, None])]
    ppermute x12 -> x0, waiting for transfers between devices: 6.72 us -> none  [the longest x6 6.58 us: extended(): after = lax.ppermute(leading, axis, down)]
  transfers between devices with their start and end apart: 12 -> 0, of which waited for: 6 -> 0; matrix products, arithmetic and copies ran while one was open for 3% -> 0% of each run, Pallas kernels for 0% -> 0%
where the time goes in v1:
time: 62.7 us; the launch traced here: 62.3 us
  Pallas kernels  53.3 us (85%)
  local copies, waits for them, and re-layouts  8.37 us (13%)
  between operations  0.66 us (1%)
    pallas_call x1, Pallas kernels, on_device(): call(links[0, 0], spread, mixing, thickness, fields.reshape(slabs, LEVELS...  53.3 us
    unnamed x15, local copies, waits for them, and re-layouts  8.37 us

profile of v1, /device:TPU:1, one launch (start us, length us, event | category | flops | bytes accessed | tf_op | source)
XLA Modules:
  0.0 62.3 jit_solution(35185309788335001)
XLA Ops:
  0.6 1.0 %copy.17 = s32[1,1,3,8100]{3,2,1,0:T(4,128)S(1)} copy(s32[1,1,3,8100]{3,1,2,0:T(1,128)} %param.8) | data formatting | bytes 194400
  1.6 1.0 %copy.16 = f32[1,1,3,8100]{3,2,1,0:T(4,128)S(1)} copy(f32[1,1,3,8100]{3,1,2,0:T(1,128)} %param.10) | data formatting | bytes 194400
  2.6 0.0 copy-start
  2.6 1.3 %copy-done = f32[1,1,3,3,4,8100]{5,4,3,2,1,0:T(4,128)S(1)} copy-done((f32[1,1,3,3,4,8100]{5,4,3,2,1,0:T(4,128)S(1)}, f32[1,1,3,3,4,8100]{5,4,3,2,1,0:T(4,128)}, u32[]{:S(2)}) %copy-start) | copy-done | bytes 1166424
  3.8 0.0 copy-start.1
  3.8 0.7 %copy-done.1 = s32[1,1,3,4,4]{4,3,2,1,0:T(4,128)S(1)} copy-done((s32[1,1,3,4,4]{4,3,2,1,0:T(4,128)S(1)}, s32[1,1,3,4,4]{4,3,2,1,0:T(4,128)}, u32[]{:S(2)}) %copy-start.1) | copy-done | bytes 216
  4.5 0.0 copy-start.2
  4.5 0.7 %copy-done.2 = f32[3,4]{1,0:T(4,128)S(1)} copy-done((f32[3,4]{1,0:T(4,128)S(1)}, f32[3,4]{1,0:T(4,128)}, u32[]{:S(2)}) %copy-start.2) | copy-done | bytes 72
  5.2 0.0 copy-start.3
  5.2 0.7 %copy-done.3 = f32[4]{0:T(128)S(1)} copy-done((f32[4]{0:T(128)S(1)}, f32[4]{0:T(128)}, u32[]{:S(2)}) %copy-start.3) | copy-done | bytes 40
  5.9 0.0 copy-start.4
  5.9 0.7 %copy-done.4 = f32[4]{0:T(128)S(1)} copy-done((f32[4]{0:T(128)S(1)}, f32[4]{0:T(128)}, u32[]{:S(2)}) %copy-start.4) | copy-done | bytes 40
  6.5 53.3 %slab_and_gradients.1 = (f32[9,4,8100]{2,1,0:T(4,128)S(1)}, f32[3,8100]{1,0:T(4,128)S(1)}, f32[3,8100]{1,0:T(4,128)S(1)}) custom-call(s32[3,4,4]{2,1,0:T(4,128)S(1)} %bitcast.17, f32[3,4]{1,0:T(4,128)S(1)} %copy-done.2, f32[4]{0:T(128)S(1)} %copy-done.3, f32[4]{0:T(128)S(1)} %copy-done.4, f32[9,4,8100]{2,1,0:T(4,128)S(1)} %bitcast.11, ...), custom_call_target="tpu_custom_call" | custom-call | tf_op jit(solution)/shard_map/slab_and_gradients/pallas_call | solution.py:502
  59.8 0.7 %copy.10 = f32[1,1,3,8100]{3,1,2,0:T(1,128)} copy(f32[1,1,3,8100]{3,2,1,0:T(4,128)S(1)} %bitcast.16) | data formatting | bytes 194400
  60.6 0.7 %copy.11 = f32[1,1,3,8100]{3,1,2,0:T(1,128)} copy(f32[1,1,3,8100]{3,2,1,0:T(4,128)S(1)} %bitcast.15) | data formatting | bytes 194400
  61.3 1.0 %copy.19 = f32[1,1,3,3,4,8100]{5,4,3,2,1,0:T(4,128)} copy(f32[1,1,3,3,4,8100]{5,4,3,2,1,0:T(4,128)S(1)} %bitcast.12) | data formatting | bytes 2332800
Async XLA Ops:
  2.6 1.3 %copy-start = (f32[1,1,3,3,4,8100]{5,4,3,2,1,0:T(4,128)S(1)}, f32[1,1,3,3,4,8100]{5,4,3,2,1,0:T(4,128)}, u32[]{:S(2)}) copy-start(f32[1,1,3,3,4,8100]{5,4,3,2,1,0:T(4,128)} %param.7) | copy-start | bytes 3499204
  3.8 0.7 %copy-start.1 = (s32[1,1,3,4,4]{4,3,2,1,0:T(4,128)S(1)}, s32[1,1,3,4,4]{4,3,2,1,0:T(4,128)}, u32[]{:S(2)}) copy-start(s32[1,1,3,4,4]{4,3,2,1,0:T(4,128)} %param.9) | copy-start | bytes 580
  4.5 0.7 %copy-start.2 = (f32[3,4]{1,0:T(4,128)S(1)}, f32[3,4]{1,0:T(4,128)}, u32[]{:S(2)}) copy-start(f32[3,4]{1,0:T(4,128)} %spread.1) | copy-start | bytes 148
  5.2 0.7 %copy-start.3 = (f32[4]{0:T(128)S(1)}, f32[4]{0:T(128)}, u32[]{:S(2)}) copy-start(f32[4]{0:T(128)} %mixing.1) | copy-start | bytes 52
  5.9 0.7 %copy-start.4 = (f32[4]{0:T(128)S(1)}, f32[4]{0:T(128)}, u32[]{:S(2)}) copy-start(f32[4]{0:T(128)} %thickness.1) | copy-start | bytes 52

commit v2 on v1

--- a/solution.py
+++ b/solution.py
@@ -17,6 +17,7 @@
 WIDE = LANES * BLOCKS
 SPLIT = 45
 CENTRE = 5.0
+GRANT = 57_000_000
 MESH = pl.DeviceIdType.MESH
 WEST, EAST, SOUTH, NORTH = 0, 1, 2, 3
 
@@ -88,17 +89,43 @@
 
 def kernel(
     sizes,
-    links, spread, mixing, thickness, fields, wet_land, diagonal,
-    adjoint, answer, remainder,
-    raw, raw_wet, raw_diagonal, masked, stepped, wet, wet_levels, centre_term,
-    not_west, not_east, rim_mask, east_flow, north_flow, first_field, second_field, third_field,
+    links_in, spread_in, mixing_in, thickness_in, fields, wet_land, diagonal,
+    adjoint, vectors, scales,
+    raw, raw_wet, raw_diagonal, masked, stepped, vector_rows, scale_row, wet, wet_levels, centre_term,
+    not_west, not_east, rim_mask, east_flow, north_flow,
     flags, turn_a, turn_b, valid, spreads, mixings, weights,
-    rows_a, rows_b, slab_rows, answer_rows, remainder_rows,
+    rows_a, rows_b, slab_rows,
     send_1, recv_1, send_2, recv_2, send_3, recv_3, send_slab, recv_slab,
-    plane, column,
-    in_sems, out_sem, send_sems, recv_sems, hello,
+    plane, column, links, spread, mixing, thickness,
+    in_sems, out_sems, send_sems, recv_sems, hello,
 ):
     groups, strips, length = sizes
+    wet_copy = pltpu.make_async_copy(wet_land, raw_wet, in_sems.at[9])
+    wet_copy.start()
+    def field_copy(a):
+        return pltpu.make_async_copy(fields.at[a], raw.at[a], in_sems.at[a])
+
+    for k in range(SLOTS):
+        for f in range(2):
+            field_copy(k * FIELDS + f).start()
+    diagonal_copy = pltpu.make_async_copy(diagonal, raw_diagonal, in_sems.at[10])
+    diagonal_copy.start()
+    table_copies = [
+        pltpu.make_async_copy(source, target, in_sems.at[11 + i])
+        for i, (source, target) in enumerate(
+            (
+                (links_in, links),
+                (spread_in, spread),
+                (mixing_in, mixing),
+                (thickness_in, thickness),
+            )
+        )
+    ]
+    for copy in table_copies:
+        copy.start()
+    for k in range(SLOTS):
+        field_copy(k * FIELDS + 2).start()
+
     t = lax.axis_index("tiles")
     s = lax.axis_index("strip")
     core = lax.rem(t, 2)
@@ -120,88 +147,89 @@
     def column_device(offset):
         return ((x * length + lax.rem(z + offset + length, length)) * 2 + core, s)
 
-    reach = min(4, length // 2)
     near = [(dt, ds) for dt in (-1, 0, 1) for ds in (-1, 0, 1) if (dt, ds) != (0, 0)]
-    along = []
-    for d in range(1, reach + 1):
-        along += [d] if 2 * d == length else [d, -d]
+    stride = 2 * length
+
+    def offset_device(dx, ds, dz, other):
+        along_x = lax.rem(x + dx + groups // stride, groups // stride)
+        along_z = lax.rem(z + dz + length, length)
+        along_s = lax.rem(s + ds + strips, strips)
+        return ((along_x * length + along_z) * 2 + (1 - core if other else core), along_s)
+
+    first = [(1, 0, 0, 0), (-1, 0, 0, 0), (0, 0, 1, 0), (0, 0, -1, 0)]
     barrier = pltpu.get_barrier_semaphore()
     for dt, ds in near:
         pl.semaphore_signal(barrier, inc=1, device_id=beside_device(dt, ds), device_id_type=MESH)
-    for offset in along:
-        pl.semaphore_signal(barrier, inc=1, device_id=column_device(offset), device_id_type=MESH)
-    for offset in range(1, planes):
-        pl.semaphore_signal(barrier, inc=1, device_id=plane_device(offset), device_id_type=MESH)
-
-    wet_copy = pltpu.make_async_copy(wet_land, raw_wet, in_sems.at[9])
-    wet_copy.start()
-    field_copies = {}
-    for f in (0, 1, 2):
-        for k in range(SLOTS):
-            a = k * FIELDS + f
-            field_copies[a] = pltpu.make_async_copy(fields.at[a], raw.at[a], in_sems.at[a])
-            field_copies[a].start()
-    diagonal_copy = pltpu.make_async_copy(diagonal, raw_diagonal, in_sems.at[10])
-    diagonal_copy.start()
+    for offset in first:
+        pl.semaphore_signal(
+            barrier, inc=1, device_id=offset_device(*offset), device_id_type=MESH
+        )
+
+    rounds = [
+        first + [(0, 1, 0, 0), (0, -1, 0, 0), (0, 0, 0, 1), (0, 1, 0, 1), (0, -1, 0, 1)],
+        [(2, 0, 0, 0), (0, 2, 0, 0), (0, 0, 0, 1), (0, 0, 2, 0), (0, 0, -2, 0)],
+    ]
+    reach = 4
+    while reach < length // 2:
+        rounds.append([(0, 0, reach, 0), (0, 0, -reach, 0)])
+        reach *= 2
+
+    def greet(i):
+        if i < len(rounds):
+            for offset in rounds[i]:
+                pl.semaphore_signal(
+                    hello.at[i], inc=1, device_id=offset_device(*offset), device_id_type=MESH
+                )
+
+    def greeted(i):
+        if i < len(rounds):
+            pl.semaphore_wait(hello.at[i], len(rounds[i]))
 
     cell = lax.broadcasted_iota(jnp.int32, (4, WIDE), 1)
     row = lax.shift_right_logical(cell * 11651, 20)
     place = cell - row * TILE
-    not_west[...] = jnp.where(place == 0, 0.0, 1.0)
-    not_east[...] = jnp.where(place == TILE - 1, 0.0, 1.0)
     at_rim = (place == 0) | (place == TILE - 1)
     rim_mask[...] = jnp.where(at_rim & (cell < CELLS), 1.0, 0.0)
-    zero_row = jnp.zeros((1, LANES), jnp.float32)
-    for side in range(4):
-        for k in range(SLOTS):
-            code = links[k, side, 3]
-            there = (links[k, side, 2] >= 0).astype(jnp.float32)
-            one = lambda flag: flag.astype(jnp.float32)
-            fill = lambda value: jnp.full((1, LANES), value, jnp.float32)
-            flags[side, k : k + 1, :] = fill(one(code != 0))
-            valid[side, k : k + 1, :] = fill(there)
-            turn_a[side, k : k + 1, :] = fill(there * (one(code == 0) - one(code == 2)))
-            turn_b[side, k : k + 1, :] = fill(there * (one(code == 1) - one(code == 3)))
-        for table in (flags, valid, turn_a, turn_b, rows_a, rows_b):
-            table[side, 3:4, :] = zero_row
+    tail = jnp.zeros((4, LANES), jnp.float32)
+    wet[:, block(63)] = tail
+    wet[3:4, :] = jnp.zeros((1, WIDE), jnp.float32)
+    for a in range(SLOTS * FIELDS):
+        masked[a, :, block(63)] = tail
+
+    def tiled(rows):
+        return jnp.concatenate([rows] * BLOCKS, axis=1)
+
+    for copy in table_copies:
+        copy.wait()
     for l in range(LEVELS):
         weights[l : l + 1, :] = jnp.full((1, LANES), thickness[l], jnp.float32)
-        mixings[l : l + 1, :] = jnp.full((1, LANES), mixing[l], jnp.float32)
-        for f in range(FIELDS):
-            spreads[f, l : l + 1, :] = jnp.full((1, LANES), spread[f, l], jnp.float32)
-    for table in (wet, centre_term, east_flow, north_flow):
-        table[...] = jnp.zeros((4, WIDE), jnp.float32)
-    tail = jnp.zeros((4, LANES), jnp.float32)
-    for a in range(SLOTS * FIELDS):
-        masked[a, :, block(63)] = tail
-
-    def tiled(rows):
-        return jnp.concatenate([rows] * BLOCKS, axis=1)
-
     wet_copy.wait()
-    wet[0:3, 0:CELLS] = raw_wet[...].astype(jnp.float32)
     for k in range(SLOTS):
+        wet[k : k + 1, 0:CELLS] = raw_wet[k].astype(jnp.float32)
         wet_levels[k] = jnp.broadcast_to(wet[k : k + 1, :], (4, WIDE))
 
-    def mask_field(a, k):
+    rim = lambda k: rim_mask[:, block(k)]
+
+    def slab_rims(k, f):
+        a = k * FIELDS + f
+        field_copy(a).wait()
         kept = wet_levels[k, :, 0:CELLS] > 0.0
         masked[a, :, 0:CELLS] = jnp.where(kept, raw[a], 0.0)
-
-    for k in range(SLOTS):
-        for f, flow in ((0, east_flow), (1, north_flow)):
-            a = k * FIELDS + f
-            field_copies[a].wait()
-            mask_field(a, k)
-            scaled = masked[a] * tiled(weights[...])
-            flow[k : k + 1, :] = jnp.sum(scaled, axis=0, keepdims=True)
-
-    rim = lambda k: rim_mask[:, block(k)]
-    for part, flow in ((0, east_flow), (1, north_flow)):
-        for side, value in enumerate(rims_of(lambda k: flow[:, block(k)], rim)):
-            for k in range(SLOTS):
-                send_1[side, k, part : part + 1, :] = value[k : k + 1, :]
-
-    pl.semaphore_wait(barrier, len(near) + len(along) + planes - 1)
+        values = rims_of(lambda i: masked[a, :, block(i)], rim)
+        for side, value in enumerate(values):
+            send_slab[side, a] = value
+        return values
+
+    def velocity_rims(i, carry):
+        k = lax.div(i, 2)
+        f = lax.rem(i, 2)
+        for side, value in enumerate(slab_rims(k, f)):
+            send_1[side, i] = jnp.sum(value * weights[...], axis=0, keepdims=True)
+        return carry
+
+    lax.fori_loop(0, 2 * SLOTS, velocity_rims, 0)
+
+    pl.semaphore_wait(barrier, len(near) + len(first))
 
     def exchange(sent, received, slot, width):
         for d in (-1, 0, 1):
@@ -235,37 +263,46 @@
         step = jnp.clip(step, -1, 1) + 1
         return step * SLOTS + jnp.clip(links[k, side, 2], 0, SLOTS - 1)
 
-    exchange(send_1, recv_1, 0, SLOTS)
-    greeting = reach
-    rounds = []
-    while greeting < length // 2:
-        rounds.append(greeting)
-        greeting *= 2
-
-    def greet(i):
-        if i < len(rounds):
-            for offset in (rounds[i], -rounds[i]):
-                pl.semaphore_signal(
-                    hello.at[i], inc=1, device_id=column_device(offset), device_id_type=MESH
-                )
-
-    def greeted(i):
-        if i < len(rounds):
-            pl.semaphore_wait(hello.at[i], 2)
-
+    exchange(send_1, recv_1, 0, 2 * SLOTS)
     greet(0)
 
+    def scalar_rims(k, carry):
+        slab_rims(k, 2)
+        return carry
+
+    lax.fori_loop(0, SLOTS, scalar_rims, 0)
+    exchange(send_slab, recv_slab, 3, SLOTS * FIELDS)
+    greeted(0)
+    greet(1)
+
+    not_west[...] = jnp.where(place == 0, 0.0, 1.0)
+    not_east[...] = jnp.where(place == TILE - 1, 0.0, 1.0)
+    zero_row = jnp.zeros((1, LANES), jnp.float32)
+    for side in range(4):
+        for k in range(SLOTS):
+            code = links[k, side, 3]
+            there = (links[k, side, 2] >= 0).astype(jnp.float32)
+            one = lambda flag: flag.astype(jnp.float32)
+            fill = lambda value: jnp.full((1, LANES), value, jnp.float32)
+            flags[side, k : k + 1, :] = fill(one(code != 0))
+            valid[side, k : k + 1, :] = fill(there)
+            turn_a[side, k : k + 1, :] = fill(there * (one(code == 0) - one(code == 2)))
+            turn_b[side, k : k + 1, :] = fill(there * (one(code == 1) - one(code == 3)))
+        for table in (flags, valid, turn_a, turn_b, rows_a, rows_b):
+            table[side, 3:4, :] = zero_row
+    for l in range(LEVELS):
+        mixings[l : l + 1, :] = jnp.full((1, LANES), mixing[l], jnp.float32)
+        for f in range(FIELDS):
+            spreads[f, l : l + 1, :] = jnp.full((1, LANES), spread[f, l], jnp.float32)
+    centre_term[:, block(63)] = tail
+    for table in (centre_term, east_flow, north_flow):
+        table[3:4, :] = jnp.zeros((1, WIDE), jnp.float32)
     for k in range(SLOTS):
-        field_copies[k * FIELDS + 2].wait()
-        mask_field(k * FIELDS + 2, k)
-
-    def slab_rims(a, carry):
-        for side, value in enumerate(rims_of(lambda k: masked[a, :, block(k)], rim)):
-            send_slab[side, a] = value
-        return carry
-
-    lax.fori_loop(0, SLOTS * FIELDS, slab_rims, 0)
-    exchange(send_slab, recv_slab, 3, SLOTS * FIELDS)
+        for f, flow in ((0, east_flow), (1, north_flow)):
+            scaled = masked[k * FIELDS + f] * tiled(weights[...])
+            flow[k : k + 1, :] = jnp.sum(scaled, axis=0, keepdims=True)
+
+    first_field, second_field, third_field = (vector_rows.at[i] for i in range(3))
 
     def flux_inside():
         west, east, _, _ = beside(east_flow[...], not_west[...], not_east[...])
@@ -274,7 +311,8 @@
 
     first_field[...] = flux_inside()
     diagonal_copy.wait()
-    centre_term[0:3, 0:CELLS] = raw_diagonal[...] + (4.0 - CENTRE)
+    for k in range(SLOTS):
+        centre_term[k : k + 1, 0:CELLS] = raw_diagonal[k] + (4.0 - CENTRE)
 
     def add_rims(target, scale, west, east, south, north):
         columns, first, before, final = spread_rims(west, east, south, north)
@@ -307,9 +345,9 @@
     gathered = []
     for side in range(4):
         for k in range(SLOTS):
-            pair = recv_1[side, source_of(k, side)]
-            rows_a[side, k : k + 1, :] = pair[0:1, :]
-            rows_b[side, k : k + 1, :] = pair[1:2, :]
+            at = 2 * source_of(k, side)
+            rows_a[side, k : k + 1, :] = recv_1[side, at]
+            rows_b[side, k : k + 1, :] = recv_1[side, at + 1]
         a, b = turn_a[side], turn_b[side]
         if side in (WEST, EAST):
             turned = a * rows_a[side] + b * rows_b[side]
@@ -320,12 +358,14 @@
         gathered.append(flip(turned, flags[side]))
     add_rims(first_field, 0.5, *gathered)
     send_surface(first_field, send_2, recv_2, 1)
+    greeted(1)
+    greet(2)
 
     operator_inside(second_field, first_field)
     add_rims(second_field, -1.0, *received_surface(recv_2, 1))
     send_surface(second_field, send_3, recv_3, 2)
-    greeted(0)
-    greet(1)
+    greeted(2)
+    greet(3)
 
     operator_inside(third_field, second_field)
 
@@ -337,6 +377,7 @@
     moment_2 = total(second_field[...] * second_field[...])
     add_rims(third_field, -1.0, *received_surface(recv_3, 2))
     moment_3 = total(second_field[...] * third_field[...])
+    vectors_copy = pltpu.make_async_copy(vector_rows, vectors, out_sems.at[1])
     lane = lane_row((1, LANES))
     packed = jnp.where(lane == 0, moment_0, 0.0)
     packed = jnp.where(lane == 1, moment_1, packed)
@@ -359,9 +400,8 @@
         return whole(buffer.at[pl.ds(0, count)], slot)
 
     share(plane, here, packed, [plane_device(o) for o in range(1, planes)], 4)
-    for i in range(1, len(rounds)):
+    for i in range(3, len(rounds)):
         greeted(i)
-        greet(i + 1)
     shared(plane, planes - 1, 4).wait_recv()
     packed = jnp.sum(plane[...], axis=0)
     offsets = []
@@ -369,6 +409,7 @@
         offsets += [d] if 2 * d == length else [d, -d]
     share(column, z, packed, [column_device(o) for o in offsets], 5)
 
+    vectors_copy.start()
     whole(recv_slab, 3).wait_recv()
 
     def slab_orient(k, carry):
@@ -413,7 +454,7 @@
             m + tiled(spreads[f]) * flat + tiled(mixings[...]) * vertical
         )
         stepped[a] = updated[:, 0:CELLS]
-        pltpu.make_async_copy(stepped.at[a], adjoint.at[a], out_sem.at[0]).start()
+        pltpu.make_async_copy(stepped.at[a], adjoint.at[a], out_sems.at[0]).start()
         return carry
 
     lax.fori_loop(0, SLOTS * FIELDS, slab_step, 0)
@@ -431,20 +472,56 @@
     alpha_1 = beta / (applied - beta * beta * mu)
     c1 = alpha_0 + alpha_1 * (1.0 + beta)
     c2 = alpha_0 * alpha_1
-    r, v, w = first_field[...], second_field[...], third_field[...]
-    found = (c1 - CENTRE * c2) * r - c2 * v
-    left = (1.0 - CENTRE * c1 + CENTRE * CENTRE * c2) * r + (2.0 * CENTRE * c2 - c1) * v + c2 * w
-    answer_rows[...] = found[0:3, 0:CELLS]
-    remainder_rows[...] = left[0:3, 0:CELLS]
-    answer_copy = pltpu.make_async_copy(answer_rows, answer, out_sem.at[1])
-    remainder_copy = pltpu.make_async_copy(remainder_rows, remainder, out_sem.at[2])
-    answer_copy.start()
-    remainder_copy.start()
+    scale_row[...] = jnp.where(lane == 0, c1, jnp.where(lane == 1, c2, 0.0))
+    scales_copy = pltpu.make_async_copy(scale_row, scales, out_sems.at[2])
+    scales_copy.start()
     for slot, buffer in enumerate((recv_1, recv_2, recv_3, recv_slab)):
         whole(buffer, slot).wait_send()
     shared(plane, planes - 1, 4).wait_send()
     shared(column, length - 1, 5).wait_send()
-    pltpu.make_async_copy(stepped, adjoint, out_sem.at[0]).wait()
+    pltpu.make_async_copy(stepped, adjoint, out_sems.at[0]).wait()
+    vectors_copy.wait()
+    scales_copy.wait()
+
+
+def final_kernel(
+    adjoint_in, vectors_in, scales_in, adjoint, answer, remainder,
+    slab, vectors, scales, answer_rows, remainder_rows, in_sems, out_sems,
+):
+    scales_copy = pltpu.make_async_copy(scales_in, scales, in_sems.at[0])
+    scales_copy.start()
+    vectors_copy = pltpu.make_async_copy(vectors_in, vectors, in_sems.at[1])
+    vectors_copy.start()
+    slabs = SLOTS * FIELDS
+    incoming = [
+        pltpu.make_async_copy(adjoint_in.at[a], slab.at[a], in_sems.at[2 + a])
+        for a in range(slabs)
+    ]
+    outgoing = [
+        pltpu.make_async_copy(slab.at[a], adjoint.at[a], out_sems.at[2 + a])
+        for a in range(slabs)
+    ]
+    for copy in incoming:
+        copy.start()
+    scales_copy.wait()
+    vectors_copy.wait()
+    c1 = scales[0:1, 0:1]
+    c2 = scales[0:1, 1:2]
+    r, v, w = (vectors[i, 0:3, 0:CELLS] for i in range(3))
+    found = (c1 - CENTRE * c2) * r - c2 * v
+    left = (1.0 - CENTRE * c1 + CENTRE * CENTRE * c2) * r + (2.0 * CENTRE * c2 - c1) * v + c2 * w
+    for k in range(SLOTS):
+        answer_rows[k] = found[k : k + 1]
+        remainder_rows[k] = left[k : k + 1]
+    answer_copy = pltpu.make_async_copy(answer_rows, answer, out_sems.at[0])
+    remainder_copy = pltpu.make_async_copy(remainder_rows, remainder, out_sems.at[1])
+    answer_copy.start()
+    remainder_copy.start()
+    for arrived, leaving in zip(incoming, outgoing):
+        arrived.wait()
+        leaving.start()
+    for copy in outgoing:
+        copy.wait()
     answer_copy.wait()
     remainder_copy.wait()
 
@@ -455,60 +532,82 @@
     slabs = SLOTS * FIELDS
     f32 = jnp.float32
     V = lambda *shape: pltpu.VMEM(shape, f32)
-    smem = pl.BlockSpec(memory_space=pltpu.SMEM)
-    hbm = pl.BlockSpec(memory_space=pl.ANY)
+    hbm = pl.BlockSpec(memory_space=pltpu.HBM)
     call = pl.pallas_call(
         functools.partial(kernel, (groups, strips, length)),
         out_shape=(
             jax.ShapeDtypeStruct((slabs, LEVELS, CELLS), f32),
-            jax.ShapeDtypeStruct((SLOTS, CELLS), f32),
-            jax.ShapeDtypeStruct((SLOTS, CELLS), f32),
+            jax.ShapeDtypeStruct((3, 4, WIDE), f32),
+            jax.ShapeDtypeStruct((1, LANES), f32),
         ),
-        in_specs=[smem] * 4 + [hbm] * 3,
+        in_specs=[hbm] * 7,
         out_specs=(hbm, hbm, hbm),
         scratch_shapes=[
             V(slabs, LEVELS, CELLS),
-            pltpu.VMEM((SLOTS, CELLS), jnp.int32),
-            V(SLOTS, CELLS),
+            pltpu.VMEM((SLOTS, 1, CELLS), jnp.int32),
+            V(SLOTS, 1, CELLS),
             V(slabs, LEVELS, WIDE),
-            V(slabs, LEVELS, CELLS),
+            V(slabs, LEVELS, CELLS), V(3, 4, WIDE), V(1, LANES),
             V(4, WIDE),
             V(SLOTS, 4, WIDE),
             V(4, WIDE),
             V(4, WIDE), V(4, WIDE), V(4, WIDE),
-            V(4, WIDE), V(4, WIDE), V(4, WIDE), V(4, WIDE), V(4, WIDE),
+            V(4, WIDE), V(4, WIDE),
             V(4, 4, LANES), V(4, 4, LANES), V(4, 4, LANES), V(4, 4, LANES),
             V(FIELDS, 4, LANES), V(4, LANES), V(4, LANES),
             V(4, 4, LANES), V(4, 4, LANES), V(4, slabs, 4, LANES),
-            V(SLOTS, CELLS), V(SLOTS, CELLS),
-            V(4, SLOTS, 2, LANES), V(4, 3 * SLOTS, 2, LANES),
+            V(4, 2 * SLOTS, 1, LANES), V(4, 6 * SLOTS, 1, LANES),
             V(4, SLOTS, 1, LANES), V(4, 3 * SLOTS, 1, LANES),
             V(4, SLOTS, 1, LANES), V(4, 3 * SLOTS, 1, LANES),
             V(4, slabs, 4, LANES), V(4, 3 * slabs, 4, LANES),
             V(planes, 1, LANES), V(length, 1, LANES),
-            pltpu.SemaphoreType.DMA((11,)),
+            pltpu.SMEM((SLOTS, 4, 4), jnp.int32),
+            pltpu.SMEM((FIELDS, LEVELS), f32),
+            pltpu.SMEM((LEVELS,), f32),
+            pltpu.SMEM((LEVELS,), f32),
+            pltpu.SemaphoreType.DMA((15,)),
             pltpu.SemaphoreType.DMA((3,)),
             pltpu.SemaphoreType.DMA((6,)),
             pltpu.SemaphoreType.DMA((6,)),
             pltpu.SemaphoreType.REGULAR((4,)),
         ],
         compiler_params=pltpu.CompilerParams(
-            collective_id=0, has_side_effects=True, vmem_limit_bytes=24 * 1024 * 1024
+            collective_id=0, has_side_effects=True, vmem_limit_bytes=GRANT
         ),
         name="slab_and_gradients",
     )
 
+    finish = pl.pallas_call(
+        final_kernel,
+        out_shape=(
+            jax.ShapeDtypeStruct((slabs, LEVELS, CELLS), f32),
+            jax.ShapeDtypeStruct((SLOTS, 1, CELLS), f32),
+            jax.ShapeDtypeStruct((SLOTS, 1, CELLS), f32),
+        ),
+        in_specs=[hbm] * 3,
+        out_specs=(hbm, hbm, hbm),
+        scratch_shapes=[
+            V(slabs, LEVELS, CELLS), V(3, 4, WIDE), V(1, LANES),
+            V(SLOTS, 1, CELLS), V(SLOTS, 1, CELLS),
+            pltpu.SemaphoreType.DMA((2 + slabs,)),
+            pltpu.SemaphoreType.DMA((2 + slabs,)),
+        ],
+        compiler_params=pltpu.CompilerParams(vmem_limit_bytes=GRANT),
+        name="last_step",
+    )
+
     def on_device(fields, wet_land, links, surface_diagonal, spread, mixing, thickness):
-        updated, found, left = call(
-            links[0, 0],
+        updated, vectors, scales = call(
+            links.reshape(SLOTS, 4, 4),
             spread,
             mixing,
             thickness,
             fields.reshape(slabs, LEVELS, CELLS),
-            wet_land.reshape(SLOTS, CELLS),
-            surface_diagonal.reshape(SLOTS, CELLS),
+            wet_land.reshape(SLOTS, 1, CELLS),
+            surface_diagonal.reshape(SLOTS, 1, CELLS),
         )
-        return updated.reshape(fields.shape), found[None, None], left[None, None]
+        updated, found, left = finish(updated, vectors, scales)
+        return updated.reshape(fields.shape), found.reshape(wet_land.shape), left.reshape(wet_land.shape)
 
     return jax.shard_map(
         on_device,

time: 62.7 us -> 55.8 us (0.89)
  local copies, waits for them, and re-layouts: 8.37 us -> 0 us
  Pallas kernels: 53.3 us -> 55 us
    unnamed x15 -> x0, local copies, waits for them, and re-layouts: 8.37 us -> none
    pallas_call x1 -> x2, Pallas kernels: 53.3 us -> 55 us  [the longest x1 52.5 us: on_device(): call(links.reshape(SLOTS, 4, 4), spread, mixing, thickness, fields.reshap...]
where the time goes in v2:
time: 55.8 us; the launch traced here: 55.7 us
  Pallas kernels  55 us (99%)
  between operations  0.64 us (1%)
    pallas_call x1, Pallas kernels, on_device(): call(links.reshape(SLOTS, 4, 4), spread, mixing, thickness, fields.reshap...  52.5 us
    pallas_call x1, Pallas kernels, on_device(): updated, found, left = finish(updated, vectors, scales)  2.47 us

profile of v2, /device:TPU:1, one launch (start us, length us, event | category | flops | bytes accessed | tf_op | source)
XLA Modules:
  0.0 55.7 jit_solution(5549144944032828327)
XLA Ops:
  0.6 52.5 %slab_and_gradients.1 = (f32[9,4,8100]{2,1,0:T(4,128)}, f32[3,4,8192]{2,1,0:T(4,128)}, f32[1,128]{1,0:T(1,128)}) custom-call(s32[3,4,4]{2,1,0:T(4,128)} %bitcast.14, f32[3,4]{1,0:T(4,128)} %spread_in.1, f32[4]{0:T(128)} %mixing_in.1, f32[4]{0:T(128)} %thickness_in.1, f32[9,4,8100]{2,1,0:T(4,128)} %bitcast.11, s32[3,1,8100]{2,1,0:T(1,128)} %bitcast.12, ...), custom_call_target="tpu_custom_call" | custom-call | tf_op jit(solution)/shard_map/slab_and_gradients/pallas_call | solution.py:600
  53.2 2.5 %last_step.1 = (f32[9,4,8100]{2,1,0:T(4,128)}, f32[3,1,8100]{2,1,0:T(1,128)}, f32[3,1,8100]{2,1,0:T(1,128)}) custom-call(f32[9,4,8100]{2,1,0:T(4,128)} %get-tuple-element.9.adjoint_in, f32[3,4,8192]{2,1,0:T(4,128)} %get-tuple-element.10.vectors_in, f32[1,128]{1,0:T(1,128)} %get-tuple-element.11.scales_in), custom_call_target="tpu_custom_call" | custom-call | tf_op jit(solution)/shard_map/last_step/pallas_call | solution.py:609

commit v3 on v2

--- a/solution.py
+++ b/solution.py
@@ -95,8 +95,9 @@
     not_west, not_east, rim_mask, east_flow, north_flow,
     flags, turn_a, turn_b, valid, spreads, mixings, weights,
     rows_a, rows_b, slab_rows,
-    send_1, recv_1, send_2, recv_2, send_3, recv_3, send_slab, recv_slab,
-    plane, column, links, spread, mixing, thickness,
+    send_1, recv_1, send_2, recv_2, send_wet, recv_wet, send_slab, recv_slab,
+    corners, beside_links, own_rims,
+    plane, column, links, far_links, spread, mixing, thickness,
     in_sems, out_sems, send_sems, recv_sems, hello,
 ):
     groups, strips, length = sizes
@@ -123,6 +124,9 @@
     ]
     for copy in table_copies:
         copy.start()
+    own_links = beside_links.at[4]
+    own_links_copy = pltpu.make_async_copy(links_in, own_links, in_sems.at[15])
+    own_links_copy.start()
     for k in range(SLOTS):
         field_copy(k * FIELDS + 2).start()
 
@@ -166,7 +170,7 @@
         )
 
     rounds = [
-        first + [(0, 1, 0, 0), (0, -1, 0, 0), (0, 0, 0, 1), (0, 1, 0, 1), (0, -1, 0, 1)],
+        first,
         [(2, 0, 0, 0), (0, 2, 0, 0), (0, 0, 0, 1), (0, 0, 2, 0), (0, 0, -2, 0)],
     ]
     reach = 4
@@ -180,10 +184,15 @@
                 pl.semaphore_signal(
                     hello.at[i], inc=1, device_id=offset_device(*offset), device_id_type=MESH
                 )
+        if i == 0:
+            for offset in near:
+                pl.semaphore_signal(
+                    hello.at[i], inc=1, device_id=beside_device(*offset), device_id_type=MESH
+                )
 
     def greeted(i):
         if i < len(rounds):
-            pl.semaphore_wait(hello.at[i], len(rounds[i]))
+            pl.semaphore_wait(hello.at[i], len(rounds[i]) + (len(near) if i == 0 else 0))
 
     cell = lax.broadcasted_iota(jnp.int32, (4, WIDE), 1)
     row = lax.shift_right_logical(cell * 11651, 20)
@@ -264,6 +273,16 @@
         return step * SLOTS + jnp.clip(links[k, side, 2], 0, SLOTS - 1)
 
     exchange(send_1, recv_1, 0, 2 * SLOTS)
+    own_links_copy.wait()
+    for dt, ds in near:
+        pltpu.make_async_remote_copy(
+            src_ref=own_links,
+            dst_ref=beside_links.at[(1 - dt) * 3 + 1 - ds],
+            send_sem=send_sems.at[6],
+            recv_sem=recv_sems.at[6],
+            device_id=beside_device(dt, ds),
+            device_id_type=MESH,
+        ).start()
     greet(0)
 
     def scalar_rims(k, carry):
@@ -272,6 +291,10 @@
 
     lax.fori_loop(0, SLOTS, scalar_rims, 0)
     exchange(send_slab, recv_slab, 3, SLOTS * FIELDS)
+    for side, value in enumerate(rims_of(lambda i: wet[:, block(i)], rim)):
+        for k in range(SLOTS):
+            send_wet[side, k] = value[k : k + 1, :]
+    exchange(send_wet, recv_wet, 2, SLOTS)
     greeted(0)
     greet(1)
 
@@ -326,20 +349,43 @@
             centre_term[...] * values[...] - ((west + east) + (south + north))
         )
 
-    def send_surface(values, sent, received, slot):
-        for side, value in enumerate(rims_of(lambda k: values[:, block(k)], rim)):
-            for k in range(SLOTS):
-                sent[side, k] = value[k : k + 1, :]
-        exchange(sent, received, slot, SLOTS)
-
-    def received_surface(received, slot):
-        whole(received, slot).wait_recv()
+    def select(received, step, part):
         out = []
         for side in range(4):
             for k in range(SLOTS):
-                rows_a[side, k : k + 1, :] = received[side, source_of(k, side)]
+                rows_a[side, k : k + 1, :] = received[side, step * source_of(k, side) + part]
             out.append(flip(rows_a[side] * valid[side], flags[side]))
         return out
+
+    links_arrived = whole(beside_links.at[pl.ds(0, 8)], 6)
+    links_arrived.wait_recv()
+    links_copy = pltpu.make_async_copy(beside_links, far_links, in_sems.at[16])
+    links_copy.start()
+    links_copy.wait()
+    corner_of = {}
+    for k in range(SLOTS):
+        for side in range(4):
+            dt = jnp.clip(links[k, side, 0], -1, 1)
+            ds = jnp.clip(links[k, side, 1], -1, 1)
+            at = (dt + 1) * 3 + ds + 1
+            slot = jnp.clip(links[k, side, 2], 0, SLOTS - 1)
+            high = 1 if (side ^ 1) in (EAST, NORTH) else 0
+            for end in range(2):
+                beyond = (SOUTH if end == 0 else NORTH) if side in (WEST, EAST) else end
+                far = [far_links[at, slot, beyond, i] for i in range(4)]
+                place_flag = jnp.where(far[3] != 0, 1 - high, high)
+                facing = beyond ^ 1
+                if facing in (SOUTH, NORTH):
+                    lane_at = (TILE - 1 if facing == NORTH else 0) + place_flag
+                else:
+                    lane_at = (TILE - 1) * place_flag + (1 if facing == EAST else 0)
+                go_t = jnp.clip(far[0], -1, 1) + dt + 2
+                go_s = lax.rem(jnp.clip(far[1], -1, 1) + ds + 2 * strips, strips)
+                line = (go_t * strips + go_s) * SLOTS + jnp.clip(far[2], 0, SLOTS - 1)
+                corner_of[k, side, end] = (
+                    line,
+                    jnp.where(far[2] >= 0, lane_at, LANES),
+                )
 
     whole(recv_1, 0).wait_recv()
     gathered = []
@@ -357,25 +403,73 @@
             turned = -turned
         gathered.append(flip(turned, flags[side]))
     add_rims(first_field, 0.5, *gathered)
-    send_surface(first_field, send_2, recv_2, 1)
+    for side, value in enumerate(rims_of(lambda k: first_field[:, block(k)], rim)):
+        own_rims[side] = value
+        for k in range(SLOTS):
+            send_2[side, 2 * k] = value[k : k + 1, :]
+    lanes = lane_row()
+    corner_rows = jnp.where(
+        (lanes == 0) | (lanes == TILE - 1),
+        own_rims[WEST],
+        pltpu.roll(own_rims[EAST], 1, 1),
+    )
+    own_place = 2 * strips * SLOTS
+    for k in range(SLOTS):
+        corners[own_place + k] = corner_rows[k : k + 1, :]
+    far_devices = [(dt, ds) for ds in range(strips) for dt in range(-2, 3) if (dt, ds) != (0, 0)]
+    for dt, ds in far_devices:
+        pltpu.make_async_remote_copy(
+            src_ref=corners.at[pl.ds(own_place, SLOTS)],
+            dst_ref=corners.at[
+                pl.ds(((2 - dt) * strips + (strips - ds) % strips) * SLOTS, SLOTS)
+            ],
+            send_sem=send_sems.at[7],
+            recv_sem=recv_sems.at[7],
+            device_id=(lax.rem(t + dt + groups, groups), lax.rem(s + ds, strips)),
+            device_id_type=MESH,
+        ).start()
+    operator_inside(second_field, first_field)
+    for side, value in enumerate(rims_of(lambda k: second_field[:, block(k)], rim)):
+        for k in range(SLOTS):
+            send_2[side, 2 * k + 1] = value[k : k + 1, :]
+    exchange(send_2, recv_2, 1, 2 * SLOTS)
     greeted(1)
     greet(2)
 
-    operator_inside(second_field, first_field)
-    add_rims(second_field, -1.0, *received_surface(recv_2, 1))
-    send_surface(second_field, send_3, recv_3, 2)
+    def total(value):
+        return jnp.sum(jnp.sum(value, axis=1, keepdims=True), axis=0, keepdims=True)
+
+    moment_0 = total(first_field[...] * first_field[...])
+    whole(recv_wet, 2).wait_recv()
+    wet_beside = select(recv_wet, 1, 0)
+    whole(recv_2, 1).wait_recv()
+    add_rims(second_field, -1.0, *select(recv_2, 2, 0))
+    inside_beside = select(recv_2, 2, 1)
+    operator_inside(third_field, second_field)
+    corners_arrived = whole(corners.at[pl.ds(0, len(far_devices) * SLOTS)], 7)
+    corners_arrived.wait_recv()
+    line_lanes = lane_row((1, LANES))
+    image_beside = []
+    for side in range(4):
+        for k in range(SLOTS):
+            both = []
+            for end in range(2):
+                line, lane_at = corner_of[k, side, end]
+                kept = jnp.where(line_lanes == lane_at, corners[line], 0.0)
+                both.append(jnp.sum(kept, axis=1, keepdims=True))
+            rows_a[side, k : k + 1, :] = jnp.where(
+                line_lanes == 0, both[0], jnp.where(line_lanes == TILE - 1, both[1], 0.0)
+            )
+        others = flip(rows_a[side], flags[side])
+        image_beside.append(
+            inside_beside[side]
+            - wet_beside[side] * (jnp.where(lanes < TILE, own_rims[side], 0.0) + others)
+        )
+    add_rims(third_field, -1.0, *image_beside)
     greeted(2)
     greet(3)
-
-    operator_inside(third_field, second_field)
-
-    def total(value):
-        return jnp.sum(jnp.sum(value, axis=1, keepdims=True), axis=0, keepdims=True)
-
-    moment_0 = total(first_field[...] * first_field[...])
     moment_1 = total(first_field[...] * second_field[...])
     moment_2 = total(second_field[...] * second_field[...])
-    add_rims(third_field, -1.0, *received_surface(recv_3, 2))
     moment_3 = total(second_field[...] * third_field[...])
     vectors_copy = pltpu.make_async_copy(vector_rows, vectors, out_sems.at[1])
     lane = lane_row((1, LANES))
@@ -475,8 +569,10 @@
     scale_row[...] = jnp.where(lane == 0, c1, jnp.where(lane == 1, c2, 0.0))
     scales_copy = pltpu.make_async_copy(scale_row, scales, out_sems.at[2])
     scales_copy.start()
-    for slot, buffer in enumerate((recv_1, recv_2, recv_3, recv_slab)):
+    for slot, buffer in enumerate((recv_1, recv_2, recv_wet, recv_slab)):
         whole(buffer, slot).wait_send()
+    links_arrived.wait_send()
+    corners_arrived.wait_send()
     shared(plane, planes - 1, 4).wait_send()
     shared(column, length - 1, 5).wait_send()
     pltpu.make_async_copy(stepped, adjoint, out_sems.at[0]).wait()
@@ -557,18 +653,22 @@
             V(FIELDS, 4, LANES), V(4, LANES), V(4, LANES),
             V(4, 4, LANES), V(4, 4, LANES), V(4, slabs, 4, LANES),
             V(4, 2 * SLOTS, 1, LANES), V(4, 6 * SLOTS, 1, LANES),
-            V(4, SLOTS, 1, LANES), V(4, 3 * SLOTS, 1, LANES),
+            V(4, 2 * SLOTS, 1, LANES), V(4, 6 * SLOTS, 1, LANES),
             V(4, SLOTS, 1, LANES), V(4, 3 * SLOTS, 1, LANES),
             V(4, slabs, 4, LANES), V(4, 3 * slabs, 4, LANES),
+            V(5 * strips * SLOTS, 1, LANES),
+            pltpu.VMEM((9, SLOTS, 4, 4), jnp.int32),
+            V(4, 4, LANES),
             V(planes, 1, LANES), V(length, 1, LANES),
             pltpu.SMEM((SLOTS, 4, 4), jnp.int32),
+            pltpu.SMEM((9, SLOTS, 4, 4), jnp.int32),
             pltpu.SMEM((FIELDS, LEVELS), f32),
             pltpu.SMEM((LEVELS,), f32),
             pltpu.SMEM((LEVELS,), f32),
-            pltpu.SemaphoreType.DMA((15,)),
+            pltpu.SemaphoreType.DMA((17,)),
             pltpu.SemaphoreType.DMA((3,)),
-            pltpu.SemaphoreType.DMA((6,)),
-            pltpu.SemaphoreType.DMA((6,)),
+            pltpu.SemaphoreType.DMA((8,)),
+            pltpu.SemaphoreType.DMA((8,)),
             pltpu.SemaphoreType.REGULAR((4,)),
         ],
         compiler_params=pltpu.CompilerParams(

time: 55.8 us -> 54.2 us (0.971)
  Pallas kernels: 55 us -> 53.4 us
    pallas_call x1, Pallas kernels: 52.5 us -> 50.9 us  [on_device(): call(links.reshape(SLOTS, 4, 4), spread, mixing, thickness, fields.reshap...]
where the time goes in v3:
time: 54.2 us; the launch traced here: 54 us
  Pallas kernels  53.4 us (99%)
  between operations  0.64 us (1%)
    pallas_call x1, Pallas kernels, on_device(): call(links.reshape(SLOTS, 4, 4), spread, mixing, thickness, fields.reshap...  50.9 us
    pallas_call x1, Pallas kernels, on_device(): updated, found, left = finish(updated, vectors, scales)  2.47 us

profile of v3, /device:TPU:1, one launch (start us, length us, event | category | flops | bytes accessed | tf_op | source)
XLA Modules:
  0.0 54.0 jit_solution(17236607999941061923)
XLA Ops:
  0.6 50.9 %slab_and_gradients.1 = (f32[9,4,8100]{2,1,0:T(4,128)}, f32[3,4,8192]{2,1,0:T(4,128)}, f32[1,128]{1,0:T(1,128)}) custom-call(s32[3,4,4]{2,1,0:T(4,128)} %bitcast.14, f32[3,4]{1,0:T(4,128)} %spread_in.1, f32[4]{0:T(128)} %mixing_in.1, f32[4]{0:T(128)} %thickness_in.1, f32[9,4,8100]{2,1,0:T(4,128)} %bitcast.11, s32[3,1,8100]{2,1,0:T(1,128)} %bitcast.12, ...), custom_call_target="tpu_custom_call" | custom-call | tf_op jit(solution)/shard_map/slab_and_gradients/pallas_call | solution.py:700
  51.6 2.5 %last_step.1 = (f32[9,4,8100]{2,1,0:T(4,128)}, f32[3,1,8100]{2,1,0:T(1,128)}, f32[3,1,8100]{2,1,0:T(1,128)}) custom-call(f32[9,4,8100]{2,1,0:T(4,128)} %get-tuple-element.9.adjoint_in, f32[3,4,8192]{2,1,0:T(4,128)} %get-tuple-element.10.vectors_in, f32[1,128]{1,0:T(1,128)} %get-tuple-element.11.scales_in), custom_call_target="tpu_custom_call" | custom-call | tf_op jit(solution)/shard_map/last_step/pallas_call | solution.py:709

commit v4 on v3

--- a/solution.py
+++ b/solution.py
@@ -96,7 +96,7 @@
     flags, turn_a, turn_b, valid, spreads, mixings, weights,
     rows_a, rows_b, slab_rows,
     send_1, recv_1, send_2, recv_2, send_wet, recv_wet, send_slab, recv_slab,
-    corners, beside_links, own_rims,
+    corners, beside_links, own_rims, wet_rims, centre_rims, inside_rims, image_rims,
     plane, column, links, far_links, spread, mixing, thickness,
     in_sems, out_sems, send_sems, recv_sems, hello,
 ):
@@ -142,12 +142,6 @@
     def beside_device(dt, ds):
         return (lax.rem(t + dt + groups, groups), lax.rem(s + ds + strips, strips))
 
-    def plane_device(offset):
-        other = lax.rem(here + offset, planes)
-        at_x = lax.div(other, 2 * strips)
-        at_s = lax.rem(lax.div(other, 2), strips)
-        return ((at_x * length + z) * 2 + lax.rem(other, 2), at_s)
-
     def column_device(offset):
         return ((x * length + lax.rem(z + offset + length, length)) * 2 + core, s)
 
@@ -241,7 +235,7 @@
     pl.semaphore_wait(barrier, len(near) + len(first))
 
     def exchange(sent, received, slot, width):
-        for d in (-1, 0, 1):
+        for d in (-1, 1, 0):
             for side, device in (
                 (EAST, beside_device(1, d)),
                 (WEST, beside_device(-1, d)),
@@ -291,7 +285,13 @@
 
     lax.fori_loop(0, SLOTS, scalar_rims, 0)
     exchange(send_slab, recv_slab, 3, SLOTS * FIELDS)
+    lanes = lane_row()
+
+    def on_rim(rows):
+        return jnp.where(lanes < TILE, rows, 0.0)
+
     for side, value in enumerate(rims_of(lambda i: wet[:, block(i)], rim)):
+        wet_rims[side] = on_rim(value)
         for k in range(SLOTS):
             send_wet[side, k] = value[k : k + 1, :]
     exchange(send_wet, recv_wet, 2, SLOTS)
@@ -356,6 +356,46 @@
                 rows_a[side, k : k + 1, :] = received[side, step * source_of(k, side) + part]
             out.append(flip(rows_a[side] * valid[side], flags[side]))
         return out
+
+    def keep_rims(target, values):
+        for side, value in enumerate(rims_of(lambda k: values[:, block(k)], rim)):
+            target[side] = on_rim(value)
+
+    def at_ends(low, high):
+        return jnp.where(lanes == 0, low, 0.0) + jnp.where(lanes == TILE - 1, high, 0.0)
+
+    def moved(rows, start, stop):
+        return pltpu.roll(rows, (stop - start) % LANES, 1) if start != stop else rows
+
+    def corner_terms(rows, step):
+        last = TILE - 1
+        out = []
+        for side in range(4):
+            low, high = (SOUTH, NORTH) if side in (WEST, EAST) else (WEST, EAST)
+            place = step if side in (WEST, SOUTH) else last - step
+            out.append(at_ends(moved(rows[low], place, 0), moved(rows[high], place, last)))
+        return out
+
+    def rim_image(rows):
+        terms = corner_terms(rows, 1)
+        return [
+            wet_rims[side]
+            * (
+                centre_rims[side] * rows[side]
+                - (pltpu.roll(rows[side], 1, 1) + pltpu.roll(rows[side], LANES - 1, 1))
+                - terms[side]
+            )
+            for side in range(4)
+        ]
+
+    def rim_change(scale, rows):
+        terms = corner_terms(rows, 0)
+        return [scale * wet_rims[side] * (rows[side] + terms[side]) for side in range(4)]
+
+    keep_rims(centre_rims, centre_term)
+    keep_rims(own_rims, first_field)
+    operator_inside(second_field, first_field)
+    keep_rims(inside_rims, second_field)
 
     links_arrived = whole(beside_links.at[pl.ds(0, 8)], 6)
     links_arrived.wait_recv()
@@ -401,13 +441,18 @@
             turned = a * rows_b[side] - b * rows_a[side]
         if side in (WEST, SOUTH):
             turned = -turned
-        gathered.append(flip(turned, flags[side]))
-    add_rims(first_field, 0.5, *gathered)
-    for side, value in enumerate(rims_of(lambda k: first_field[:, block(k)], rim)):
-        own_rims[side] = value
+        gathered.append(on_rim(flip(turned, flags[side])))
+    change = rim_change(0.5, gathered)
+    images = rim_image(change)
+    for side in range(4):
+        rows = own_rims[side] + change[side]
+        own_rims[side] = rows
         for k in range(SLOTS):
-            send_2[side, 2 * k] = value[k : k + 1, :]
-    lanes = lane_row()
+            send_2[side, 2 * k] = rows[k : k + 1, :]
+        rows = inside_rims[side] + images[side]
+        inside_rims[side] = rows
+        for k in range(SLOTS):
+            send_2[side, 2 * k + 1] = rows[k : k + 1, :]
     corner_rows = jnp.where(
         (lanes == 0) | (lanes == TILE - 1),
         own_rims[WEST],
@@ -417,6 +462,7 @@
     for k in range(SLOTS):
         corners[own_place + k] = corner_rows[k : k + 1, :]
     far_devices = [(dt, ds) for ds in range(strips) for dt in range(-2, 3) if (dt, ds) != (0, 0)]
+    far_devices.sort(key=lambda o: -abs(o[0]) // 2 - min(o[1], strips - o[1]))
     for dt, ds in far_devices:
         pltpu.make_async_remote_copy(
             src_ref=corners.at[pl.ds(own_place, SLOTS)],
@@ -428,10 +474,6 @@
             device_id=(lax.rem(t + dt + groups, groups), lax.rem(s + ds, strips)),
             device_id_type=MESH,
         ).start()
-    operator_inside(second_field, first_field)
-    for side, value in enumerate(rims_of(lambda k: second_field[:, block(k)], rim)):
-        for k in range(SLOTS):
-            send_2[side, 2 * k + 1] = value[k : k + 1, :]
     exchange(send_2, recv_2, 1, 2 * SLOTS)
     greeted(1)
     greet(2)
@@ -439,13 +481,23 @@
     def total(value):
         return jnp.sum(jnp.sum(value, axis=1, keepdims=True), axis=0, keepdims=True)
 
+    add_rims(first_field, 0.5, *gathered)
+    operator_inside(second_field, first_field)
+    operator_inside(third_field, second_field)
+    keep_rims(image_rims, third_field)
     moment_0 = total(first_field[...] * first_field[...])
+    moment_1 = total(first_field[...] * second_field[...])
+    moment_2 = total(second_field[...] * second_field[...])
+    moment_3 = total(second_field[...] * third_field[...])
     whole(recv_wet, 2).wait_recv()
     wet_beside = select(recv_wet, 1, 0)
+    greeted(2)
+    greet(3)
     whole(recv_2, 1).wait_recv()
-    add_rims(second_field, -1.0, *select(recv_2, 2, 0))
+    others_beside = [on_rim(rows) for rows in select(recv_2, 2, 0)]
     inside_beside = select(recv_2, 2, 1)
-    operator_inside(third_field, second_field)
+    change = rim_change(-1.0, others_beside)
+    images = rim_image(change)
     corners_arrived = whole(corners.at[pl.ds(0, len(far_devices) * SLOTS)], 7)
     corners_arrived.wait_recv()
     line_lanes = lane_row((1, LANES))
@@ -463,14 +515,25 @@
         others = flip(rows_a[side], flags[side])
         image_beside.append(
             inside_beside[side]
-            - wet_beside[side] * (jnp.where(lanes < TILE, own_rims[side], 0.0) + others)
+            - wet_beside[side] * (own_rims[side] + others)
         )
-    add_rims(third_field, -1.0, *image_beside)
-    greeted(2)
-    greet(3)
-    moment_1 = total(first_field[...] * second_field[...])
-    moment_2 = total(second_field[...] * second_field[...])
-    moment_3 = total(second_field[...] * third_field[...])
+    between = (lanes > 0) & (lanes < TILE - 1)
+    sums = [jnp.zeros((4, LANES), jnp.float32)] * 3
+    for side in range(4):
+        once = change[side]
+        if side in (SOUTH, NORTH):
+            once = jnp.where(between, once, 0.0)
+        found = inside_rims[side] + change[side]
+        sums = [
+            sums[0] + once * own_rims[side],
+            sums[1] + once * (inside_rims[side] + found),
+            sums[2]
+            + once * (2.0 * image_rims[side] + images[side])
+            - found * on_rim(image_beside[side]),
+        ]
+    moment_1 += total(sums[0])
+    moment_2 += total(sums[1])
+    moment_3 += total(sums[2])
     vectors_copy = pltpu.make_async_copy(vector_rows, vectors, out_sems.at[1])
     lane = lane_row((1, LANES))
     packed = jnp.where(lane == 0, moment_0, 0.0)
@@ -493,7 +556,20 @@
     def shared(buffer, count, slot):
         return whole(buffer.at[pl.ds(0, count)], slot)
 
-    share(plane, here, packed, [plane_device(o) for o in range(1, planes)], 4)
+    across = groups // stride
+
+    def hops(step, count):
+        return min(step, count - step)
+
+    in_plane = [
+        (dx, ds, 0, other)
+        for dx in range(across)
+        for ds in range(strips)
+        for other in (0, 1)
+        if (dx, ds, other) != (0, 0, 0)
+    ]
+    in_plane.sort(key=lambda o: -hops(o[0], across) - hops(o[1], strips))
+    share(plane, here, packed, [offset_device(*o) for o in in_plane], 4)
     for i in range(3, len(rounds)):
         greeted(i)
     shared(plane, planes - 1, 4).wait_recv()
@@ -503,6 +579,9 @@
         offsets += [d] if 2 * d == length else [d, -d]
     share(column, z, packed, [column_device(o) for o in offsets], 5)
 
+    add_rims(second_field, -1.0, *others_beside)
+    operator_inside(third_field, second_field)
+    add_rims(third_field, -1.0, *image_beside)
     vectors_copy.start()
     whole(recv_slab, 3).wait_recv()
 
@@ -658,7 +737,7 @@
             V(4, slabs, 4, LANES), V(4, 3 * slabs, 4, LANES),
             V(5 * strips * SLOTS, 1, LANES),
             pltpu.VMEM((9, SLOTS, 4, 4), jnp.int32),
-            V(4, 4, LANES),
+            V(4, 4, LANES), V(4, 4, LANES), V(4, 4, LANES), V(4, 4, LANES), V(4, 4, LANES),
             V(planes, 1, LANES), V(length, 1, LANES),
             pltpu.SMEM((SLOTS, 4, 4), jnp.int32),
             pltpu.SMEM((9, SLOTS, 4, 4), jnp.int32),

time: 54.2 us -> 53.3 us (0.983)
  Pallas kernels: 53.4 us -> 52.5 us
    pallas_call x1, Pallas kernels: 50.9 us -> 50 us  [on_device(): call(links.reshape(SLOTS, 4, 4), spread, mixing, thickness, fields.reshap...]
where the time goes in v4:
time: 53.3 us; the launch traced here: 53.1 us
  Pallas kernels  52.5 us (98%)
  between operations  0.64 us (1%)
    pallas_call x1, Pallas kernels, on_device(): call(links.reshape(SLOTS, 4, 4), spread, mixing, thickness, fields.reshap...  50 us
    pallas_call x1, Pallas kernels, on_device(): updated, found, left = finish(updated, vectors, scales)  2.47 us

profile of v4, /device:TPU:1, one launch (start us, length us, event | category | flops | bytes accessed | tf_op | source)
XLA Modules:
  0.0 53.1 jit_solution(8615746069094625630)
XLA Ops:
  0.6 50.0 %slab_and_gradients.1 = (f32[9,4,8100]{2,1,0:T(4,128)}, f32[3,4,8192]{2,1,0:T(4,128)}, f32[1,128]{1,0:T(1,128)}) custom-call(s32[3,4,4]{2,1,0:T(4,128)} %bitcast.14, f32[3,4]{1,0:T(4,128)} %spread_in.1, f32[4]{0:T(128)} %mixing_in.1, f32[4]{0:T(128)} %thickness_in.1, f32[9,4,8100]{2,1,0:T(4,128)} %bitcast.11, s32[3,1,8100]{2,1,0:T(1,128)} %bitcast.12, ...), custom_call_target="tpu_custom_call" | custom-call | tf_op jit(solution)/shard_map/slab_and_gradients/pallas_call | solution.py:779
  50.6 2.5 %last_step.1 = (f32[9,4,8100]{2,1,0:T(4,128)}, f32[3,1,8100]{2,1,0:T(1,128)}, f32[3,1,8100]{2,1,0:T(1,128)}) custom-call(f32[9,4,8100]{2,1,0:T(4,128)} %get-tuple-element.9.adjoint_in, f32[3,4,8192]{2,1,0:T(4,128)} %get-tuple-element.10.vectors_in, f32[1,128]{1,0:T(1,128)} %get-tuple-element.11.scales_in), custom_call_target="tpu_custom_call" | custom-call | tf_op jit(solution)/shard_map/last_step/pallas_call | solution.py:788

commit v5 on v4

--- a/solution.py
+++ b/solution.py
@@ -101,16 +101,6 @@
     in_sems, out_sems, send_sems, recv_sems, hello,
 ):
     groups, strips, length = sizes
-    wet_copy = pltpu.make_async_copy(wet_land, raw_wet, in_sems.at[9])
-    wet_copy.start()
-    def field_copy(a):
-        return pltpu.make_async_copy(fields.at[a], raw.at[a], in_sems.at[a])
-
-    for k in range(SLOTS):
-        for f in range(2):
-            field_copy(k * FIELDS + f).start()
-    diagonal_copy = pltpu.make_async_copy(diagonal, raw_diagonal, in_sems.at[10])
-    diagonal_copy.start()
     table_copies = [
         pltpu.make_async_copy(source, target, in_sems.at[11 + i])
         for i, (source, target) in enumerate(
@@ -124,6 +114,16 @@
     ]
     for copy in table_copies:
         copy.start()
+    wet_copy = pltpu.make_async_copy(wet_land, raw_wet, in_sems.at[9])
+    wet_copy.start()
+    def field_copy(a):
+        return pltpu.make_async_copy(fields.at[a], raw.at[a], in_sems.at[a])
+
+    for k in range(SLOTS):
+        for f in range(2):
+            field_copy(k * FIELDS + f).start()
+    diagonal_copy = pltpu.make_async_copy(diagonal, raw_diagonal, in_sems.at[10])
+    diagonal_copy.start()
     own_links = beside_links.at[4]
     own_links_copy = pltpu.make_async_copy(links_in, own_links, in_sems.at[15])
     own_links_copy.start()
@@ -498,10 +498,33 @@
     inside_beside = select(recv_2, 2, 1)
     change = rim_change(-1.0, others_beside)
     images = rim_image(change)
+    between = (lanes > 0) & (lanes < TILE - 1)
+    sums = [jnp.zeros((4, LANES), jnp.float32)] * 3
+    found = []
+    for side in range(4):
+        once = change[side]
+        if side in (SOUTH, NORTH):
+            once = jnp.where(between, once, 0.0)
+        rows = inside_rims[side] + change[side]
+        found.append(rows)
+        image = inside_beside[side] - wet_beside[side] * own_rims[side]
+        sums = [
+            sums[0] + once * own_rims[side],
+            sums[1] + once * (inside_rims[side] + rows),
+            sums[2] + once * (2.0 * image_rims[side] + images[side]) - rows * on_rim(image),
+        ]
+    lane = lane_row((1, LANES))
+    moment_1 += total(sums[0])
+    moment_2 += total(sums[1])
+    packed = jnp.where(lane == 0, moment_0, 0.0)
+    packed = jnp.where(lane == 1, moment_1, packed)
+    packed = jnp.where(lane == 2, moment_2, packed)
+    moment_3 += total(sums[2])
     corners_arrived = whole(corners.at[pl.ds(0, len(far_devices) * SLOTS)], 7)
     corners_arrived.wait_recv()
     line_lanes = lane_row((1, LANES))
     image_beside = []
+    crossed = jnp.zeros((4, LANES), jnp.float32)
     for side in range(4):
         for k in range(SLOTS):
             both = []
@@ -512,34 +535,13 @@
             rows_a[side, k : k + 1, :] = jnp.where(
                 line_lanes == 0, both[0], jnp.where(line_lanes == TILE - 1, both[1], 0.0)
             )
-        others = flip(rows_a[side], flags[side])
+        others = wet_beside[side] * flip(rows_a[side], flags[side])
+        crossed = crossed + found[side] * on_rim(others)
         image_beside.append(
-            inside_beside[side]
-            - wet_beside[side] * (own_rims[side] + others)
+            inside_beside[side] - wet_beside[side] * own_rims[side] - others
         )
-    between = (lanes > 0) & (lanes < TILE - 1)
-    sums = [jnp.zeros((4, LANES), jnp.float32)] * 3
-    for side in range(4):
-        once = change[side]
-        if side in (SOUTH, NORTH):
-            once = jnp.where(between, once, 0.0)
-        found = inside_rims[side] + change[side]
-        sums = [
-            sums[0] + once * own_rims[side],
-            sums[1] + once * (inside_rims[side] + found),
-            sums[2]
-            + once * (2.0 * image_rims[side] + images[side])
-            - found * on_rim(image_beside[side]),
-        ]
-    moment_1 += total(sums[0])
-    moment_2 += total(sums[1])
-    moment_3 += total(sums[2])
+    packed = jnp.where(lane == 3, moment_3 + total(crossed), packed)
     vectors_copy = pltpu.make_async_copy(vector_rows, vectors, out_sems.at[1])
-    lane = lane_row((1, LANES))
-    packed = jnp.where(lane == 0, moment_0, 0.0)
-    packed = jnp.where(lane == 1, moment_1, packed)
-    packed = jnp.where(lane == 2, moment_2, packed)
-    packed = jnp.where(lane == 3, moment_3, packed)
 
     def share(buffer, position, value, devices, slot):
         buffer[position] = value
@@ -664,9 +666,7 @@
     slab, vectors, scales, answer_rows, remainder_rows, in_sems, out_sems,
 ):
     scales_copy = pltpu.make_async_copy(scales_in, scales, in_sems.at[0])
-    scales_copy.start()
     vectors_copy = pltpu.make_async_copy(vectors_in, vectors, in_sems.at[1])
-    vectors_copy.start()
     slabs = SLOTS * FIELDS
     incoming = [
         pltpu.make_async_copy(adjoint_in.at[a], slab.at[a], in_sems.at[2 + a])
@@ -676,8 +676,15 @@
         pltpu.make_async_copy(slab.at[a], adjoint.at[a], out_sems.at[2 + a])
         for a in range(slabs)
     ]
-    for copy in incoming:
+    for copy in incoming[:4]:
         copy.start()
+    scales_copy.start()
+    vectors_copy.start()
+    for copy in incoming[4:]:
+        copy.start()
+    for arrived, leaving in zip(incoming[:4], outgoing[:4]):
+        arrived.wait()
+        leaving.start()
     scales_copy.wait()
     vectors_copy.wait()
     c1 = scales[0:1, 0:1]
@@ -692,7 +699,7 @@
     remainder_copy = pltpu.make_async_copy(remainder_rows, remainder, out_sems.at[1])
     answer_copy.start()
     remainder_copy.start()
-    for arrived, leaving in zip(incoming, outgoing):
+    for arrived, leaving in zip(incoming[4:], outgoing[4:]):
         arrived.wait()
         leaving.start()
     for copy in outgoing:

time: 53.3 us -> 53.4 us (level)
  no operation moved by 1% of the time
where the time goes in v5:
time: 53.4 us; the launch traced here: 53.2 us
  Pallas kernels  52.6 us (99%)
  between operations  0.64 us (1%)
    pallas_call x1, Pallas kernels, on_device(): call(links.reshape(SLOTS, 4, 4), spread, mixing, thickness, fields.reshap...  50 us
    pallas_call x1, Pallas kernels, on_device(): updated, found, left = finish(updated, vectors, scales)  2.56 us

profile of v5, /device:TPU:1, one launch (start us, length us, event | category | flops | bytes accessed | tf_op | source)
XLA Modules:
  0.0 53.2 jit_solution(16344279484321537209)
XLA Ops:
  0.6 50.0 %slab_and_gradients.1 = (f32[9,4,8100]{2,1,0:T(4,128)}, f32[3,4,8192]{2,1,0:T(4,128)}, f32[1,128]{1,0:T(1,128)}) custom-call(s32[3,4,4]{2,1,0:T(4,128)} %bitcast.14, f32[3,4]{1,0:T(4,128)} %spread_in.1, f32[4]{0:T(128)} %mixing_in.1, f32[4]{0:T(128)} %thickness_in.1, f32[9,4,8100]{2,1,0:T(4,128)} %bitcast.11, s32[3,1,8100]{2,1,0:T(1,128)} %bitcast.12, ...), custom_call_target="tpu_custom_call" | custom-call | tf_op jit(solution)/shard_map/slab_and_gradients/pallas_call | solution.py:786
  50.7 2.6 %last_step.1 = (f32[9,4,8100]{2,1,0:T(4,128)}, f32[3,1,8100]{2,1,0:T(1,128)}, f32[3,1,8100]{2,1,0:T(1,128)}) custom-call(f32[9,4,8100]{2,1,0:T(4,128)} %get-tuple-element.9.adjoint_in, f32[3,4,8192]{2,1,0:T(4,128)} %get-tuple-element.10.vectors_in, f32[1,128]{1,0:T(1,128)} %get-tuple-element.11.scales_in), custom_call_target="tpu_custom_call" | custom-call | tf_op jit(solution)/shard_map/last_step/pallas_call | solution.py:795
